TPU v7x, 32 devices: a whole 2x2x4 slice. The times are simulated.
32 devices in a mesh: dp: 16 (over z, y, core), seq: 2 (over x).
Axes of the slice: x: 2, y: 2, z: 4, core: 2. Of those that a mesh axis runs over, the one named last changes fastest.
Arguments:
- tokens: bfloat16 [64, 128, 1536], P(('dp', 'seq')), may hold values from -6 to 6
- cotangent: bfloat16 [64, 128, 1536], P(('dp', 'seq')), may hold values from -6 to 6
- w_query: bfloat16 [1536, 1536], P('dp'), may hold values from -0.15625 to 0.15625
- w_key: bfloat16 [1536, 768], P('dp'), may hold values from -0.15625 to 0.15625
- w_value: bfloat16 [1536, 768], P('dp'), may hold values from -0.15625 to 0.15625
- w_out: bfloat16 [1536, 1536], P('dp'), may hold values from -0.625 to 0.625
- w_gate: bfloat16 [1536, 4096], P('dp'), may hold values from -0.15625 to 0.15625
- w_up: bfloat16 [1536, 4096], P('dp'), may hold values from -0.15625 to 0.15625
- w_down: bfloat16 [4096, 1536], P('dp'), may hold values from -0.09375 to 0.09375
- gain_attn: bfloat16 [1536], P('dp'), may hold values from 0.5 to 1.5
- gain_mlp: bfloat16 [1536], P('dp'), may hold values from 0.5 to 1.5
Outputs:
- block_out: bfloat16 [64, 128, 1536], P(('dp', 'seq'))
- grad_tokens: bfloat16 [64, 128, 1536], P(('dp', 'seq'))
- grad_query: float32 [1536, 1536], P('dp')
- grad_key: float32 [1536, 768], P('dp')
- grad_value: float32 [1536, 768], P('dp')
- grad_out: float32 [1536, 1536], P('dp')
- grad_gate: float32 [1536, 4096], P('dp')
- grad_up: float32 [1536, 4096], P('dp')
- grad_down: float32 [4096, 1536], P('dp')
- grad_gain_attn: float32 [1536], P('dp')
- grad_gain_mlp: float32 [1536], P('dp')
All inputs are finite; a program needn't handle non-finite values.
Results may differ from a plain program's by a relative error of at most 0.015.
Values may be sent and summed in bfloat16 or wider, within the bound.
A program may use at most 256 MiB of HBM per device.

v0:
```python
import jax
import jax.numpy as jnp
import numpy as np
from jax import lax
from jax.experimental import pallas as pl
from jax.experimental.pallas import tpu as pltpu
from jax.sharding import PartitionSpec as P

HD = 96
EPS = 1e-05
THETA = 100000.0


def rotary(positions, width):
    steps_half = jnp.arange(width // 2, dtype=jnp.float32)
    frequency = jnp.power(THETA, -2.0 * steps_half / width)
    angles = positions[:, None] * frequency[None, :]
    cosine = jnp.cos(angles)
    sine = jnp.sin(angles)
    return (jnp.concatenate([cosine, cosine], -1), jnp.concatenate([sine, sine], -1))


def rotate(values, cosine, sine):
    half = values.shape[-1] // 2
    turned = jnp.concatenate([-values[..., half:], values[..., :half]], -1)
    return values * cosine[:, None, :] + turned * sine[:, None, :]


def rotate_back(grads, cosine, sine):
    half = grads.shape[-1] // 2
    sined = grads * sine[:, None, :]
    turned = jnp.concatenate([sined[..., half:], -sined[..., :half]], -1)
    return grads * cosine[:, None, :] + turned


def dot32(left, right):
    return jnp.dot(left, right, preferred_element_type=jnp.float32)


def dot_t(left, right):
    return lax.dot_general(left, right, (((1,), (1,)), ((), ())), preferred_element_type=jnp.float32)


def dot_l(left, right):
    return lax.dot_general(left, right, (((0,), (0,)), ((), ())), preferred_element_type=jnp.float32)


def inv_rms(values):
    return lax.rsqrt(jnp.mean(values * values, axis=-1, keepdims=True) + EPS)


def low(values):
    return values.astype(jnp.bfloat16)


def attend(queries, keys, values):
    rows = queries.shape[1]
    ids = jnp.arange(rows, dtype=jnp.int32)
    visible = ids[:, None] >= ids[None, :]
    scores = HD ** (-0.5) * jnp.einsum("bqkgd,bckd->bkgqc", queries, keys, preferred_element_type=jnp.float32)
    scores = jnp.where(visible, scores, -jnp.inf)
    top = jnp.max(scores, -1, keepdims=True)
    exps = jnp.exp(scores - top)
    probs = exps / jnp.sum(exps, -1, keepdims=True)
    mixed = jnp.einsum("bkgqc,bckd->bqkgd", low(probs), values, preferred_element_type=jnp.float32)
    return probs, low(mixed)


def attend_back(queries, keys, values, probs, grad_mixed):
    grad_values = jnp.einsum("bkgqc,bqkgd->bckd", low(probs), grad_mixed, preferred_element_type=jnp.float32)
    grad_probs = jnp.einsum("bqkgd,bckd->bkgqc", grad_mixed, values, preferred_element_type=jnp.float32)
    grad_scores = low(probs * (grad_probs - jnp.sum(probs * grad_probs, -1, keepdims=True)))
    scale = HD ** (-0.5)
    grad_queries = scale * jnp.einsum("bkgqc,bckd->bqkgd", grad_scores, keys, preferred_element_type=jnp.float32)
    grad_keys = scale * jnp.einsum("bkgqc,bqkgd->bckd", grad_scores, queries, preferred_element_type=jnp.float32)
    return grad_queries, grad_keys, grad_values


def mlp_grads(gate, up, grad_hidden):
    sigma = jax.nn.sigmoid(gate)
    silu = gate * sigma
    hidden = low(silu * up)
    grad_gate = low(grad_hidden * up * sigma * (1.0 + gate * (1.0 - sigma)))
    grad_up = low(grad_hidden * silu)
    return hidden, grad_gate, grad_up


def shards_plain(tokens, cotangent, w_query, w_key, w_value, w_out, w_gate, w_up, w_down, gain_attn, gain_mlp):
    seqs, length, width = tokens.shape
    rows = seqs * length
    kv_heads = w_key.shape[1] // HD
    groups = w_query.shape[1] // w_key.shape[1]
    gather = lambda w: lax.all_gather(w, "dp", axis=0, tiled=True)
    full_query, full_key, full_value, full_out = map(gather, (w_query, w_key, w_value, w_out))
    gains = gather(jnp.stack([gain_attn, gain_mlp], 1)).astype(jnp.float32)
    gain_one, gain_two = gains[:, 0], gains[:, 1]
    full_gate, full_up, full_down = map(gather, (w_gate, w_up, w_down))
    cosine, sine = rotary(jnp.arange(length, dtype=jnp.float32), HD)
    cosine, sine = jnp.tile(cosine, (seqs, 1)), jnp.tile(sine, (seqs, 1))

    inputs = tokens.reshape(rows, width).astype(jnp.float32)
    grad_in = cotangent.reshape(rows, width)
    scale_one = inv_rms(inputs)
    normed = low(inputs * scale_one * gain_one)
    queries = low(rotate(dot32(normed, full_query).reshape(rows, -1, HD), cosine, sine))
    keys = low(rotate(dot32(normed, full_key).reshape(rows, -1, HD), cosine, sine))
    values = low(dot32(normed, full_value))
    queries = queries.reshape(seqs, length, kv_heads, groups, HD)
    keys = keys.reshape(seqs, length, kv_heads, HD)
    values = values.reshape(seqs, length, kv_heads, HD)
    probs, mixed = attend(queries, keys, values)
    mixed = mixed.reshape(rows, -1)
    hidden_one = inputs + dot32(mixed, full_out)
    scale_two = inv_rms(hidden_one)
    normed_two = low(hidden_one * scale_two * gain_two)
    gate, up = dot32(normed_two, full_gate), dot32(normed_two, full_up)
    hidden, grad_gate, grad_up = mlp_grads(gate, up, dot_t(grad_in, full_down))
    block_out = low(hidden_one + dot32(hidden, full_down))

    acc_down = dot_l(hidden, grad_in)
    acc_gate = dot_l(normed_two, grad_gate)
    acc_up = dot_l(normed_two, grad_up)
    grad_normed_two = dot_t(grad_gate, full_gate) + dot_t(grad_up, full_up)
    acc_gain_two = jnp.sum(grad_normed_two * hidden_one * scale_two, 0)
    weighted = grad_normed_two * gain_two
    grad_one = grad_in.astype(jnp.float32) + scale_two * (
        weighted - hidden_one * scale_two * scale_two * jnp.mean(weighted * hidden_one, -1, keepdims=True)
    )
    grad_branch = low(grad_one)
    acc_out = dot_l(mixed, grad_branch)
    grad_mixed = low(dot_t(grad_branch, full_out)).reshape(queries.shape)
    grad_queries, grad_keys, grad_values = attend_back(queries, keys, values, probs, grad_mixed)
    grad_queries = low(rotate_back(grad_queries.reshape(rows, -1, HD), cosine, sine)).reshape(rows, -1)
    grad_keys = low(rotate_back(grad_keys.reshape(rows, -1, HD), cosine, sine)).reshape(rows, -1)
    grad_values = low(grad_values).reshape(rows, -1)
    acc_query = dot_l(normed, grad_queries)
    acc_key = dot_l(normed, grad_keys)
    acc_value = dot_l(normed, grad_values)
    grad_normed = dot_t(grad_queries, full_query) + dot_t(grad_keys, full_key) + dot_t(grad_values, full_value)
    acc_gain_one = jnp.sum(grad_normed * inputs * scale_one, 0)
    weighted = grad_normed * gain_one
    grad_tokens = grad_one + scale_one * (
        weighted - inputs * scale_one * scale_one * jnp.mean(weighted * inputs, -1, keepdims=True)
    )

    def share(acc):
        owned = lax.psum_scatter(low(acc), "dp", scatter_dimension=0, tiled=True)
        return lax.psum(owned, "seq").astype(jnp.float32)

    grads = [share(a) for a in (acc_down, acc_gate, acc_up, acc_out, acc_query, acc_key, acc_value)]
    gain_grads = lax.psum(
        lax.psum_scatter(jnp.stack([acc_gain_one, acc_gain_two], 1), "dp", scatter_dimension=0, tiled=True), "seq"
    )
    down, gate, up, out, query, key, value = grads
    return (
        block_out.reshape(tokens.shape),
        low(grad_tokens).reshape(tokens.shape),
        query, key, value, out, gate, up, down,
        gain_grads[:, 0], gain_grads[:, 1],
    )


ROWS = P(("dp", "seq"), None, None)
SPLIT = P("dp", None)
IN_SPECS = (ROWS, ROWS) + (SPLIT,) * 7 + (P("dp"), P("dp"))
OUT_SPECS = (ROWS, ROWS) + (SPLIT,) * 7 + (P("dp"), P("dp"))


MESH = pl.DeviceIdType.MESH
VMEM = pl.BlockSpec(memory_space=pltpu.VMEM)
ANY = pl.BlockSpec(memory_space=pl.ANY)
BF = jnp.bfloat16
F32 = jnp.float32
STRIP = 16
PIECES = 4
VMEM_BYTES = 66_000_000


class Place:
    def __init__(self, planes):
        self.planes = planes
        d = lax.axis_index("dp")
        self.d, self.s = d, lax.axis_index("seq")
        self.c, self.y, self.z = d % 2, (d // 2) % 2, d // 4
        self.p = d // 2
        self.rank = 2 * self.s + self.c
        self.core = (d + 1 - 2 * self.c, self.s)
        self.across = (d, 1 - self.s)
        self.corner = (d + 1 - 2 * self.c, 1 - self.s)
        self.side = (d + 2 - 4 * self.y, self.s)
        self.right = (lax.rem(d + 4, 4 * planes), self.s)
        self.left = (lax.rem(d + 4 * planes - 4, 4 * planes), self.s)
        self.has_right, self.has_left = self.z < planes - 1, self.z > 0
        odd = self.z % 2
        self.twin = self.z + 1 - 2 * odd
        self.buddy = (d + 4 - 8 * odd, self.s)


def greet(me):
    barrier = pltpu.get_barrier_semaphore()
    for peer in (me.core, me.across, me.corner, me.side, me.right, me.left):
        pl.semaphore_signal(barrier, inc=1, device_id=peer, device_id_type=MESH)
    pl.semaphore_wait(barrier, 6)


def push(src, dst, send, recv, peer):
    return pltpu.make_async_remote_copy(
        src_ref=src, dst_ref=dst, send_sem=send, recv_sem=recv, device_id=peer, device_id_type=MESH
    )


def arrived(dst, recv, peer):
    push(dst, dst, recv, recv, peer).wait_recv()


def left_over(src, send, peer):
    push(src, src, send, send, peer).wait_send()


class Slots:
    def __init__(self, ref, rows):
        self.ref, self.rows = ref, rows
        self.at = self

    def __getitem__(self, block):
        return self.ref.at[pl.ds(pl.multiple_of(block * self.rows, self.rows), self.rows)]


def group_start(me, src, dst, send, recv):
    push(src, dst.at[me.rank], send.at[0], recv.at[0], me.core).start()
    push(src, dst.at[me.rank], send.at[1], recv.at[1], me.across).start()


def group_relay(me, dst, send, recv):
    slot = dst.at[2 * (1 - me.s) + me.c]
    arrived(slot, recv.at[1], me.across)
    push(slot, slot, send.at[2], recv.at[2], me.core).start()


def group_finish(me, src, dst, send, recv):
    arrived(dst.at[2 * me.s + 1 - me.c], recv.at[0], me.core)
    arrived(dst.at[2 * (1 - me.s) + 1 - me.c], recv.at[2], me.core)
    left_over(src, send.at[0], me.core)
    left_over(src, send.at[1], me.across)
    slot = dst.at[2 * (1 - me.s) + me.c]
    left_over(slot, send.at[2], me.core)


def group_sems():
    return [pltpu.SemaphoreType.DMA((3,)), pltpu.SemaphoreType.DMA((3,))]


def upper(slot):
    return slot.at[pl.ds(0, slot.shape[0] // 2)]


def lower(slot):
    return slot.at[pl.ds(slot.shape[0] // 2, slot.shape[0] // 2)]


def line_start(me, dst, sems):
    line_side(me, dst, sems)
    line_ends(me, dst, sems)


def line_side(me, dst, sems):
    to_right, to_left, line, to_side, side, twin = sems
    slot = dst(me.p)
    push(slot, slot, to_side.at[me.z], side.at[me.z], me.side).start()


def line_ends(me, dst, sems):
    to_right, to_left, line, to_side, side, twin = sems
    slot = dst(me.p)

    @pl.when(me.has_right)
    def _():
        push(slot, slot, to_right.at[me.z], line.at[me.z], me.right).start()

    @pl.when(me.has_left)
    def _():
        push(slot, slot, to_left.at[me.z], line.at[me.z], me.left).start()


def line_hop(me, dst, sems, hop):
    to_right, to_left, line, to_side, side, twin = sems

    def pass_on(item, back, forth, may, sends):
        slot = dst(2 * item + me.y)
        arrived(slot, line.at[item], back)

        @pl.when(may)
        def _():
            push(slot, slot, sends.at[item], line.at[item], forth).start()

        if hop > 1:
            push(slot, slot, to_side.at[item], side.at[item], me.side).start()
        else:

            @pl.when(item != me.twin)
            def _():
                push(slot, slot, to_side.at[item], side.at[item], me.side).start()

            @pl.when(item == me.twin)
            def _():
                half = upper(slot)
                push(half, half, to_side.at[item], side.at[item], me.side).start()

    @pl.when(me.z >= hop)
    def _():
        pass_on(me.z - hop, me.left, me.right, me.has_right, to_right)

    @pl.when(me.z + hop < me.planes)
    def _():
        pass_on(me.z + hop, me.right, me.left, me.has_left, to_left)


def line_twin(me, dst, sems):
    to_right, to_left, line, to_side, side, twin = sems
    slot = dst(2 * me.z + 1 - me.y)
    arrived(slot, side.at[me.z], me.side)
    half = lower(slot)
    push(half, half, twin.at[0], twin.at[1], me.buddy).start()


def line_finish(me, dst, sems):
    to_right, to_left, line, to_side, side, twin = sems
    for item in range(me.planes):
        slot, mine = dst(2 * item + 1 - me.y), dst(2 * item + me.y)

        @pl.when(item == me.twin)
        def _():
            arrived(upper(slot), side.at[item], me.side)
            arrived(lower(slot), twin.at[1], me.buddy)
            left_over(upper(mine), to_side.at[item], me.side)

        @pl.when(jnp.logical_and(item != me.twin, item != me.z))
        def _():
            arrived(slot, side.at[item], me.side)

        @pl.when(item != me.twin)
        def _():
            left_over(mine, to_side.at[item], me.side)

        @pl.when(item == me.z)
        def _():
            left_over(lower(slot), twin.at[0], me.buddy)

        @pl.when(jnp.logical_and(me.has_right, item <= me.z))
        def _():
            left_over(mine, to_right.at[item], me.right)

        @pl.when(jnp.logical_and(me.has_left, item >= me.z))
        def _():
            left_over(mine, to_left.at[item], me.left)


def line_sems(planes):
    return [pltpu.SemaphoreType.DMA((planes,))] * 5 + [pltpu.SemaphoreType.DMA((2,))]


def pick(table, index):
    value = jnp.int32(table[0])
    for i in range(1, len(table)):
        value = jnp.where(index == i, table[i], value)
    return value


def far_first(planes):
    return [sorted(range(planes), key=lambda i, z=z: (-abs(i - z), i)) for z in range(planes)]


def add_into(dst, *others):
    rows = dst.shape[0]

    def body(i, carry):
        strip = pl.ds(pl.multiple_of(i * STRIP, STRIP), STRIP)
        total = dst[strip, :].astype(F32)
        for other in others:
            total = total + other[strip, :].astype(F32)
        dst[strip, :] = total.astype(dst.dtype)
        return carry

    lax.fori_loop(0, rows // STRIP, body, 0)


def reduce_start(me, own, half, sems):
    to_side, side, twin = sems[0], sems[1], sems[6]
    orders = far_first(me.planes)
    away = lower(own(2 * me.twin + 1 - me.y))
    push(away, lower(half.at[me.z]), twin.at[0], twin.at[1], me.buddy).start()
    for i in range(me.planes):
        item = pick([o[i] for o in orders], me.z)
        src, dst = own(2 * item + 1 - me.y), half.at[item]

        @pl.when(item == me.twin)
        def _():
            push(upper(src), upper(dst), to_side.at[item], side.at[item], me.side).start()

        @pl.when(jnp.logical_and(item != me.twin, item != me.z))
        def _():
            push(src, dst, to_side.at[item], side.at[item], me.side).start()


def reduce_mix(me, own, half, sems):
    to_side, side, twin = sems[0], sems[1], sems[6]
    mixed, got = own(2 * me.z + 1 - me.y), lower(half.at[me.twin])
    arrived(got, twin.at[1], me.buddy)
    add_into(lower(mixed), got)
    push(mixed, half.at[me.z], to_side.at[me.z], side.at[me.z], me.side).start()


def reduce_y(me, own, half, lines, sems, i):
    to_side, side, to_right, to_left, left, right, twin = sems
    item = pick([o[i] for o in far_first(me.planes)], me.z)
    mine, ours = half.at[item], own(2 * item + me.y)

    @pl.when(item == me.twin)
    def _():
        arrived(upper(mine), side.at[item], me.side)
        add_into(upper(mine), upper(ours))
        copy_into(lower(mine), lower(ours))

    @pl.when(item != me.twin)
    def _():
        arrived(mine, side.at[item], me.side)
        add_into(mine, ours)

    @pl.when(jnp.logical_and(item > me.z, jnp.logical_not(me.has_left)))
    def _():
        push(mine, lines.at[item], to_right.at[item], left.at[item], me.right).start()

    @pl.when(jnp.logical_and(item < me.z, jnp.logical_not(me.has_right)))
    def _():
        there = jnp.where(item == me.z - 1, me.planes, item)
        push(mine, lines.at[there], to_left.at[item], right.at[item], me.left).start()


def reduce_z(me, half, lines, sems, i):
    to_side, side, to_right, to_left, left, right, twin = sems
    item = pick([o[i] for o in far_first(me.planes)], me.z)
    mine = half.at[item]
    spot = jnp.where(item == me.z, me.planes, item)

    @pl.when(jnp.logical_and(me.has_left, item >= me.z))
    def _():
        arrived(lines.at[item], left.at[item], me.left)
        add_into(mine, lines.at[item])

        @pl.when(item > me.z)
        def _():
            push(mine, lines.at[item], to_right.at[item], left.at[item], me.right).start()

    @pl.when(jnp.logical_and(me.has_right, item <= me.z))
    def _():
        arrived(lines.at[spot], right.at[item], me.right)
        add_into(mine, lines.at[spot])

        @pl.when(item < me.z)
        def _():
            there = jnp.where(item == me.z - 1, me.planes, item)
            push(mine, lines.at[there], to_left.at[item], right.at[item], me.left).start()


def reduce_finish(me, own, half, sems):
    to_side, side, to_right, to_left, left, right, twin = sems
    left_over(lower(own(2 * me.twin + 1 - me.y)), twin.at[0], me.buddy)
    for item in range(me.planes):
        sent = own(2 * item + 1 - me.y)

        @pl.when(item == me.twin)
        def _():
            left_over(upper(sent), to_side.at[item], me.side)

        @pl.when(item != me.twin)
        def _():
            left_over(sent, to_side.at[item], me.side)

        @pl.when(item > me.z)
        def _():
            left_over(half.at[item], to_right.at[item], me.right)

        @pl.when(item < me.z)
        def _():
            left_over(half.at[item], to_left.at[item], me.left)


def reduce_sems(planes):
    return [pltpu.SemaphoreType.DMA((planes,))] * 6 + [pltpu.SemaphoreType.DMA((2,))]


def copy_into(dst, src):
    def body(i, carry):
        strip = pl.ds(pl.multiple_of(i * STRIP, STRIP), STRIP)
        dst[strip, :] = src[strip, :]
        return carry

    lax.fori_loop(0, dst.shape[0] // STRIP, body, 0)


def reduce_buffers(planes, rows, columns):
    return [pltpu.VMEM((planes, rows, columns), BF), pltpu.VMEM((planes + 1, rows, columns), BF)]


def by_chip(ref, rows=None):
    if rows is None:
        return lambda chip: ref.at[chip]
    return lambda chip: ref.at[pl.ds(pl.multiple_of(chip * rows, STRIP), rows)]


def deal_start(me, final, rows, out, local, send, recv):
    mine = out.at[me.rank]
    part = lambda core: final.at[pl.ds(pl.multiple_of(core * rows, rows), rows)]
    pltpu.make_async_copy(part(me.c), mine, local).start()
    push(part(1 - me.c), mine, send.at[0], recv.at[0], me.core).start()
    push(part(me.c), mine, send.at[1], recv.at[1], me.across).start()
    push(part(1 - me.c), mine, send.at[2], recv.at[2], me.corner).start()


def deal_finish(me, final, rows, out, local, send, recv):
    part = lambda core: final.at[pl.ds(pl.multiple_of(core * rows, rows), rows)]
    pltpu.make_async_copy(part(me.c), out.at[me.rank], local).wait()
    left_over(part(1 - me.c), send.at[0], me.core)
    left_over(part(me.c), send.at[1], me.across)
    left_over(part(1 - me.c), send.at[2], me.corner)
    arrived(out.at[2 * me.s + 1 - me.c], recv.at[0], me.core)
    arrived(out.at[2 * (1 - me.s) + me.c], recv.at[1], me.across)
    arrived(out.at[2 * (1 - me.s) + 1 - me.c], recv.at[2], me.corner)


def blocks_start(me, part, got, send, recv, i):
    seq = (1 - me.s, me.s)[i]
    push(part.at[2 * seq + 1 - me.c], got.at[seq], send.at[i], recv.at[i], me.core).start()


def blocks_cross(me, part, got, last, send, recv):
    away = 1 - me.s
    arrived(got.at[away], recv.at[0], me.core)
    add_into(got.at[away], part.at[2 * away + me.c])
    push(got.at[away], last, send.at[2], recv.at[2], me.across).start()


def blocks_finish(me, part, got, last, send, recv):
    arrived(got.at[me.s], recv.at[1], me.core)
    arrived(last, recv.at[2], me.across)
    for i, seq in enumerate((1 - me.s, me.s)):
        left_over(part.at[2 * seq + 1 - me.c], send.at[i], me.core)
    left_over(got.at[1 - me.s], send.at[2], me.across)


def blocks_sems():
    return [pltpu.SemaphoreType.DMA((3,))] * 2


def blocks_buffers(rows, width):
    return [pltpu.VMEM((2, rows, width), BF), pltpu.VMEM((rows, width), BF)]


def strips(rows, body):
    def step(i, carry):
        body(pl.ds(pl.multiple_of(i * STRIP, STRIP), STRIP))
        return carry

    lax.fori_loop(0, rows // STRIP, step, 0)


def comm_call(kernel, ident, outs, out_specs, ins, scratch, name):
    return pl.pallas_call(
        kernel,
        out_shape=outs,
        in_specs=[spec for spec, _ in ins],
        out_specs=out_specs,
        scratch_shapes=scratch,
        name=name,
        compiler_params=pltpu.CompilerParams(
            collective_id=ident, has_side_effects=True, vmem_limit_bytes=VMEM_BYTES
        ),
    )(*[value for _, value in ins])


def shape(dims, dtype=BF):
    return jax.ShapeDtypeStruct(dims, dtype)


def split_start(me, parts, dst, keep, send, recv):
    pltpu.make_async_copy(parts.at[me.c], dst(me.c), keep).start()
    push(parts.at[1 - me.c], dst(me.c), send, recv, me.core).start()


def split_finish(me, parts, dst, keep, send, recv):
    pltpu.make_async_copy(parts.at[me.c], dst(me.c), keep).wait()
    arrived(dst(1 - me.c), recv, me.core)
    left_over(parts.at[1 - me.c], send, me.core)


def norm_back(values, weighted, base):
    scale = inv_rms(values)
    return base + scale * (
        weighted - values * scale * scale * jnp.mean(weighted * values, -1, keepdims=True)
    )


LANES = 128


def head_tables(length):
    steps = np.arange(HD // 2, dtype=np.float64)
    angles = np.arange(length, dtype=np.float64)[:, None] * np.power(THETA, -2.0 * steps / HD)[None, :]
    cosine, sine, none = np.cos(angles), np.sin(angles), np.zeros_like(angles)
    tables = [(cosine, cosine), (none, sine), (-sine, none)]
    pad = ((0, 0), (0, LANES - HD))
    return np.stack([np.pad(np.concatenate(t, 1), pad) for t in tables]).astype(np.float32)


def turn(values, tables, sign):
    other = pltpu.roll(values, HD // 2, 1) * tables[1] + pltpu.roll(values, LANES - HD // 2, 1) * tables[2]
    return values * tables[0] + sign * other


def block_step(planes, length, tokens, cot, w_query, w_key, w_value, w_out, w_gate, w_up, w_down, gain_attn, gain_mlp):
    rows, width = tokens.shape
    total = 4 * rows
    depth = w_query.shape[0]
    head = w_out.shape[0]
    q_own, k_own = w_query.shape[1] // 4, w_key.shape[1] // 4
    q_cols = q_own + 2 * k_own
    block = w_down.shape[0] // 2
    units = 2 * planes * block
    half_units = units // 2
    cols = 2 * half_units
    tile, chunk = 2 * rows, 256
    heads4 = 4 * head
    piece = 2 * head // PIECES

    def kernel(x_ref, g_loc, wq_ref, wk_ref, wv_ref, out_loc, gate_ref, up_ref, down_ref, ga_ref, gm_ref, tab_ref,
               bo_ref, gx_ref, qkv_out, out_out, gu_out, dn_out, stash, *scr):
        it = iter(scr)
        take = lambda k: [next(it) for _ in range(k)]
        n_buf, g_all, qkv_all, out_all, gu_all, dn_all, heads, mixed = take(8)
        part, out_part, x1, mid, dgu, g_gu, dx_all = take(7)
        (got, last), (got_f, last_f) = take(2), take(2)
        gu_buf, dn_buf, q_buf, o_buf = [take(2), take(2)], take(2), take(2), take(3)
        n_sems, g_sems, m_sems, d_sems = take(2), take(2), take(2), take(2)
        x_sems, b_sems, f_sems, h_sems = take(2), take(2), take(2), take(2)
        q_split, gu_split = take(3), [take(3), take(3)]
        q_line, gu_line, dn_line = take(6), [take(6), take(6)], take(6)
        gu_sems, dn_sems, q_sems = [take(7), take(7)], take(7), take(7)
        gu_deal, dn_deal, q_deal, o_deal = [take(3), take(3)], take(3), take(3), take(3)
        local, edge, o_fan, o_red, fetch, sel_ref, gains = take(7)
        me = Place(planes)
        greet(me)
        tok = lambda ref: Slots(ref, rows)
        q_slots, dn_slots = by_chip(qkv_all, 2 * depth), by_chip(dn_all, block)
        gu_slots = [by_chip(gu_all.at[h], 2 * depth) for h in range(2)]

        def core_rows(ref):
            return lambda core: ref.at[pl.ds(pl.multiple_of((2 * me.p + core) * depth, STRIP), depth)]

        fetch_x = pltpu.make_async_copy(x_ref, last_f, local.at[4])
        fetch_x.start()
        stage = out_part.at[pl.ds(0, depth)]
        heads_in = []
        for i, (ref, spot, size) in enumerate(
            ((wq_ref, 0, 2 * q_own), (wk_ref, 2 * q_own, 2 * k_own), (wv_ref, 2 * q_own + 2 * k_own, 2 * k_own))
        ):
            src = ref.at[:, pl.ds(pl.multiple_of(me.s * size, LANES), size)]
            heads_in.append(pltpu.make_async_copy(src, stage.at[:, pl.ds(spot, size)], fetch.at[i]))
            heads_in[-1].start()

        q_share = q_buf[0].at[0, pl.ds(0, depth)]
        gu_share = [mid.at[pl.ds(h * depth, depth)] for h in range(2)]
        units_in = []
        for other in range(2):
            core = (me.c, 1 - me.c)[other]
            for h in range(2):
                dst = (core_rows(gu_all.at[h])(me.c), gu_share[h])[other]
                for k in range(2 * planes):
                    ref = (gate_ref, up_ref)[k // planes]
                    chip = h * planes + k % planes
                    first = (2 * chip + core) * 2 * block + me.s * block
                    copy = pltpu.make_async_copy(
                        ref.at[:, pl.ds(pl.multiple_of(first, LANES), block)],
                        dst.at[:, pl.ds(k * block, block)],
                        fetch.at[3 + (other * 2 + h) * 2 * planes + k],
                    )
                    copy.start()
                    units_in.append(copy)
        own_down = down_ref.at[pl.ds(pl.multiple_of(me.s * block, STRIP), block)]
        keep_d = pltpu.make_async_copy(own_down, dn_slots(me.p), local.at[2])
        keep_d.start()
        keep_g = pltpu.make_async_copy(g_loc, tok(g_all).at[me.rank], local.at[3])
        keep_g.start()

        same = lax.broadcasted_iota(jnp.int32, (depth, depth), 0) == lax.broadcasted_iota(jnp.int32, (depth, depth), 1)
        for k, ref in enumerate((ga_ref, gm_ref)):
            column = jnp.sum(jnp.where(same, ref[...].astype(F32), 0.0), 1, keepdims=True)
            gains[k] = jnp.broadcast_to(column, (depth, LANES))
        row = lax.broadcasted_iota(jnp.int32, (heads4, 4 * LANES), 0)
        lane = lax.broadcasted_iota(jnp.int32, (heads4, 4 * LANES), 1)
        shift = sum(jnp.where(row >= k * HD, LANES - HD, 0) for k in range(1, 4))
        sel_ref[...] = jnp.where(lane == row + shift, 1.0, 0.0).astype(BF)

        for copy in heads_in:
            copy.wait()
        gain = gains[0][:, 0:1]
        tiles = lambda first, count: [
            stage[:, first + k * LANES:first + (k + 1) * LANES].astype(F32) * gain for k in range(count)
        ]
        queries = tiles(0, 6)
        k0, k1, k2 = tiles(2 * q_own, 3)
        v0, v1, v2 = tiles(2 * q_own + 2 * k_own, 3)
        rolled = lambda value: pltpu.roll(value, LANES // 2, 1)
        in_low = lax.broadcasted_iota(jnp.int32, (depth, LANES), 1) < LANES // 2
        join = lambda first, second: jnp.where(in_low, first, second)
        shares = (
            queries[:3] + [k0, join(k1, rolled(v0)), join(rolled(v0), rolled(v1))],
            queries[3:] + [join(rolled(k1), rolled(k2)), join(rolled(k2), v1), v2],
        )
        for core in range(2):
            value = low(jnp.concatenate(shares[core], 1))

            @pl.when(me.c == core)
            def _():
                core_rows(qkv_all)(me.c)[...] = value

            @pl.when(me.c != core)
            def _():
                q_share[...] = value

        push(q_share, core_rows(qkv_all)(me.c), q_split[1], q_split[2], me.core).start()
        here = me.s == me.z // 2
        owner = me.z == me.rank
        lender = jnp.logical_and(here, jnp.logical_not(owner))
        half = lambda y: out_all.at[pl.ds(pl.multiple_of(y * 2 * head, STRIP), 2 * head)]
        head_rows = lambda core: out_all.at[pl.ds(pl.multiple_of((2 * me.y + core) * head, STRIP), head)]
        keep_o = pltpu.make_async_copy(out_loc, head_rows(me.c), local.at[1])

        @pl.when(owner)
        def _():
            keep_o.start()

        @pl.when(lender)
        def _():
            push(out_loc, head_rows(me.c), edge.at[0], edge.at[1], me.core).start()

        fetch_x.wait()

        def first_norm(strip):
            value = last_f[strip, :].astype(F32)
            n_buf[pl.ds(pl.multiple_of(me.rank * rows + strip.start, STRIP), STRIP), :] = low(value * inv_rms(value))

        strips(rows, first_norm)
        group_start(me, tok(n_buf).at[me.rank], tok(n_buf), *n_sems)
        arrived(core_rows(qkv_all)(1 - me.c), q_split[2], me.core)
        line_start(me, q_slots, q_line)

        for copy in units_in:
            copy.wait()

        def weigh(i, carry):
            strip = pl.ds(pl.multiple_of(i * STRIP, STRIP), STRIP)
            gain = gains[1, strip, 0:1]
            for h in range(2):
                for ref in (core_rows(gu_all.at[h])(me.c), gu_share[h]):
                    ref[strip, :] = low(ref[strip, :].astype(F32) * gain)
            return carry

        lax.fori_loop(0, depth // STRIP, weigh, 0)
        for h in range(2):
            push(gu_share[h], core_rows(gu_all.at[h])(me.c), gu_split[h][1], gu_split[h][2], me.core).start()
        group_start(me, g_loc, tok(g_all), *g_sems)

        fan_in, fan_right, fan_left, fan_side, fan_other = [o_fan.at[k] for k in range(5)]
        bit = lambda y, q: out_all.at[pl.ds(pl.multiple_of(y * 2 * head + q * piece, STRIP), piece)]
        go_right = jnp.logical_and(me.z >= me.rank, me.has_right)
        go_left = jnp.logical_and(me.z <= me.rank, me.has_left)

        def fan(q):
            mine = bit(me.y, q)

            @pl.when(me.z > me.rank)
            def _():
                arrived(mine, fan_in.at[q], me.left)

            @pl.when(me.z < me.rank)
            def _():
                arrived(mine, fan_in.at[q], me.right)

            @pl.when(go_right)
            def _():
                push(mine, mine, fan_right.at[q], fan_in.at[q], me.right).start()

            @pl.when(go_left)
            def _():
                push(mine, mine, fan_left.at[q], fan_in.at[q], me.left).start()

            push(mine, mine, fan_side.at[q], fan_other.at[q], me.side).start()

        @pl.when(owner)
        def _():
            keep_o.wait()
            arrived(head_rows(1 - me.c), edge.at[1], me.core)

        @pl.when(lender)
        def _():
            left_over(out_loc, edge.at[0], me.core)

        line_hop(me, q_slots, q_line, 1)
        line_twin(me, q_slots, q_line)
        fan(0)
        line_hop(me, q_slots, q_line, 2)
        group_relay(me, tok(n_buf), *n_sems)
        fan(1)
        for hop in range(3, planes):
            line_hop(me, q_slots, q_line, hop)
        fan(2)
        fan(3)
        arrived(core_rows(gu_all.at[0])(1 - me.c), gu_split[0][2], me.core)
        line_start(me, gu_slots[0], gu_line[0])
        keep_d.wait()
        line_start(me, dn_slots, dn_line)
        arrived(core_rows(gu_all.at[1])(1 - me.c), gu_split[1][2], me.core)
        group_finish(me, tok(n_buf).at[me.rank], tok(n_buf), *n_sems)
        left_over(q_share, q_split[1], me.core)
        for h in range(2):
            left_over(gu_share[h], gu_split[h][1], me.core)
        saved = pltpu.make_async_copy(n_buf, stash, local.at[0])
        saved.start()
        line_finish(me, q_slots, q_line)

        def widen(i, carry):
            feats = pl.ds(pl.multiple_of(i * tile, tile), tile)
            for k in range(2):
                g_gu[feats, k * 4 * LANES:(k + 1) * 4 * LANES] = low(
                    dot32(qkv_all[feats, k * heads4:(k + 1) * heads4], sel_ref[...])
                )
            return carry

        lax.fori_loop(0, width // tile, widen, 0)

        def project(i, carry):
            toks = pl.ds(pl.multiple_of(i * length, length), length)
            n = n_buf[toks, :]
            tabs = [tab_ref[k] for k in range(3)]
            for k in range(8):
                value = dot32(n, g_gu[:, k * LANES:(k + 1) * LANES])
                heads[toks, k * LANES:(k + 1) * LANES] = low(turn(value, tabs, 1.0) if k < 6 else value)
            return carry

        lax.fori_loop(0, total // length, project, 0)
        line_hop(me, gu_slots[0], gu_line[0], 1)
        group_relay(me, tok(g_all), *g_sems)
        line_hop(me, dn_slots, dn_line, 1)
        line_twin(me, gu_slots[0], gu_line[0])
        line_twin(me, dn_slots, dn_line)
        saved.wait()
        for q in range(PIECES):
            arrived(bit(1 - me.y, q), fan_other.at[q], me.side)

        def pair(toks, j, ref, start):
            first = start + 2 * j * LANES
            return jnp.concatenate(
                [ref[toks, first:first + LANES], ref[toks, first + LANES:first + 2 * LANES]], 0
            )

        def probabilities(toks, j):
            q = pair(toks, j, heads, 0)
            k = heads[toks, (4 + j) * LANES:(5 + j) * LANES]
            scores = HD ** (-0.5) * dot_t(q, k)
            row = lax.rem(lax.broadcasted_iota(jnp.int32, scores.shape, 0), length)
            col = lax.broadcasted_iota(jnp.int32, scores.shape, 1)
            scores = jnp.where(row >= col, scores, -jnp.inf)
            exps = jnp.exp(scores - jnp.max(scores, 1, keepdims=True))
            return q, k, exps / jnp.sum(exps, 1, keepdims=True)

        def attend_rows(first):
            def one(i, carry):
                toks = pl.ds(pl.multiple_of(first + i * length, length), length)
                outs = []
                for j in range(2):
                    _, _, p = probabilities(toks, j)
                    o = low(dot32(low(p), heads[toks, (6 + j) * LANES:(7 + j) * LANES]))
                    outs += [o[:length], o[length:]]
                mixed[toks, :] = low(dot_t(jnp.concatenate(outs, 1), sel_ref[...]))
                return carry

            lax.fori_loop(0, rows // length, one, 0)
            toks = pl.ds(pl.multiple_of(first, rows), rows)
            part[toks, :] = low(dot32(mixed[toks, :], out_all[...]))

        away, home = 1 - me.s, me.s
        attend_rows((2 * away + 1 - me.c) * rows)
        blocks_start(me, tok(part), got, *x_sems, 0)
        line_hop(me, gu_slots[0], gu_line[0], 2)
        line_ends(me, gu_slots[1], gu_line[1])
        attend_rows((2 * away + me.c) * rows)
        blocks_cross(me, tok(part), got, last, *x_sems)
        line_hop(me, dn_slots, dn_line, 2)
        attend_rows((2 * home + 1 - me.c) * rows)
        blocks_start(me, tok(part), got, *x_sems, 1)
        line_side(me, gu_slots[1], gu_line[1])
        attend_rows((2 * home + me.c) * rows)
        for hop in range(3, planes):
            line_hop(me, gu_slots[0], gu_line[0], hop)
        line_hop(me, gu_slots[1], gu_line[1], 1)
        blocks_finish(me, tok(part), got, last, *x_sems)

        def mine(strip):
            return pl.ds(pl.multiple_of(me.rank * rows + strip.start, STRIP), STRIP)

        def summed(strip, whole, some, rest):
            return (
                whole[mine(strip), :].astype(F32)
                + some[me.s, strip, :].astype(F32)
                + rest[strip, :].astype(F32)
            )

        def middle(strip):
            value = last_f[strip, :].astype(F32) + summed(strip, part, got, last)
            x1[strip, :] = value
            n_buf[mine(strip), :] = low(value * inv_rms(value))

        strips(rows, middle)
        group_start(me, tok(n_buf).at[me.rank], tok(n_buf), *m_sems)
        for hop in range(3, planes):
            line_hop(me, dn_slots, dn_line, hop)
        line_hop(me, gu_slots[1], gu_line[1], 2)
        line_twin(me, gu_slots[1], gu_line[1])
        keep_g.wait()
        group_finish(me, g_loc, tok(g_all), *g_sems)
        for q in range(PIECES):
            left_over(bit(me.y, q), fan_side.at[q], me.side)

            @pl.when(go_right)
            def _():
                left_over(bit(me.y, q), fan_right.at[q], me.right)

            @pl.when(go_left)
            def _():
                left_over(bit(me.y, q), fan_left.at[q], me.left)

        group_relay(me, tok(n_buf), *m_sems)
        group_finish(me, tok(n_buf).at[me.rank], tok(n_buf), *m_sems)
        line_finish(me, gu_slots[0], gu_line[0])
        line_finish(me, dn_slots, dn_line)

        def activations(h, j):
            first = h * half_units + j * chunk

            def step(t, carry):
                toks = pl.ds(pl.multiple_of(t * tile, tile), tile)
                n, g = n_buf[toks, :], g_all[toks, :]
                gate = dot32(n, gu_all[h, :, j * chunk:(j + 1) * chunk])
                up = dot32(n, gu_all[h, :, half_units + j * chunk:half_units + (j + 1) * chunk])
                grad = dot_t(g, dn_all[first:first + chunk, :])
                hidden, d_gate, d_up = mlp_grads(gate, up, grad)
                mid[toks, first:first + chunk] = hidden
                dgu[h, toks, j * chunk:(j + 1) * chunk] = d_gate
                dgu[h, toks, half_units + j * chunk:half_units + (j + 1) * chunk] = d_up
                return carry

            lax.fori_loop(0, total // tile, step, 0)

        def weight_grads(h, out):
            def step(i, carry):
                feats = pl.ds(pl.multiple_of(i * chunk, chunk), chunk)
                out[feats, :] = low(dot_l(n_buf[:, feats], dgu[h]))
                return carry

            lax.fori_loop(0, width // chunk, step, 0)

        steps = half_units // chunk
        for j in range(steps):
            activations(0, j)
        for hop in range(3, planes):
            line_hop(me, gu_slots[1], gu_line[1], hop)
        weight_grads(0, g_gu)
        own_gu = [by_chip(g_gu, 2 * depth), gu_slots[0]]
        reduce_start(me, own_gu[0], gu_buf[0][0], gu_sems[0])
        line_finish(me, gu_slots[1], gu_line[1])
        for j in range(steps):
            activations(1, j)
        finals = [gu_buf[h][0].at[me.z] for h in range(2)]
        gu_y = lambda h, i: reduce_y(me, own_gu[h], *gu_buf[h], gu_sems[h], i)
        gu_z = lambda h, i: reduce_z(me, *gu_buf[h], gu_sems[h], i)
        gu_mix = lambda h: reduce_mix(me, own_gu[h], gu_buf[h][0], gu_sems[h])
        dn_y = lambda i: reduce_y(me, dn_slots, *dn_buf, dn_sems, i)
        dn_z = lambda i: reduce_z(me, *dn_buf, dn_sems, i)
        q_y = lambda i: reduce_y(me, q_slots, *q_buf, q_sems, i)
        q_z = lambda i: reduce_z(me, *q_buf, q_sems, i)
        gu_mix(0)

        def back(seq):
            toks = pl.ds(pl.multiple_of(seq * tile, tile), tile)

            def step(i, carry):
                feats = pl.ds(pl.multiple_of(i * chunk, chunk), chunk)
                value = dot_t(dgu[0, toks, :], gu_all[0, feats, :]) + dot_t(dgu[1, toks, :], gu_all[1, feats, :])
                part[toks, feats] = low(value)
                return carry

            lax.fori_loop(0, width // chunk, step, 0)

        back(away)
        blocks_start(me, tok(part), got, *b_sems, 0)
        gu_y(0, 0)
        back(home)
        blocks_start(me, tok(part), got, *b_sems, 1)
        blocks_cross(me, tok(part), got, last, *b_sems)

        weight_grads(1, gu_all.at[0])
        fetch_n = pltpu.make_async_copy(stash, n_buf, local.at[0])
        fetch_n.start()
        reduce_start(me, own_gu[1], gu_buf[1][0], gu_sems[1])
        gu_y(0, 1)
        gu_z(0, 0)
        gu_y(0, 2)

        def forth(i, carry):
            feats = pl.ds(pl.multiple_of(i * chunk, chunk), chunk)
            out_part[:, feats] = low(dot32(mid[...], dn_all[:, feats]))
            return carry

        lax.fori_loop(0, width // chunk, forth, 0)
        for i in range(2):
            blocks_start(me, tok(out_part), got_f, *f_sems, i)
        gu_z(0, 1)
        gu_z(0, 2)
        gu_y(0, 3)
        blocks_finish(me, tok(part), got, last, *b_sems)

        def branch(strip):
            grad = norm_back(x1[strip, :], summed(strip, part, got, last), g_all[mine(strip), :].astype(F32))
            dx_all[mine(strip), :] = low(grad)

        strips(rows, branch)
        group_start(me, tok(dx_all).at[me.rank], tok(dx_all), *d_sems)
        gu_mix(1)

        def down(i, carry):
            these = pl.ds(pl.multiple_of(i * chunk, chunk), chunk)
            dn_all[these, :] = low(dot_l(mid[:, these], g_all[...]))
            return carry

        lax.fori_loop(0, units // chunk, down, 0)
        reduce_start(me, dn_slots, dn_buf[0], dn_sems)
        gu_z(0, 3)
        gu_y(1, 0)
        gu_y(1, 1)
        gu_z(1, 0)
        gu_y(1, 2)
        reduce_mix(me, dn_slots, dn_buf[0], dn_sems)
        group_relay(me, tok(dx_all), *d_sems)
        deal_start(me, finals[0], depth, gu_out.at[0], *gu_deal[0])
        blocks_cross(me, tok(out_part), got_f, last_f, *f_sems)
        gu_z(1, 1)
        gu_z(1, 2)
        group_finish(me, tok(dx_all).at[me.rank], tok(dx_all), *d_sems)

        def spread_out(t, carry):
            toks = pl.ds(pl.multiple_of(t * rows, rows), rows)
            grad = low(dot_t(dx_all[toks, :], out_all[...]))
            mid[toks, 0:4 * LANES] = low(dot32(grad, sel_ref[...]))
            return carry

        lax.fori_loop(0, 4, spread_out, 0)
        out_all[...] = low(dot_l(mixed[...], dx_all[...]))
        for q in range(PIECES):
            push(bit(1 - me.y, q), o_buf[0].at[pl.ds(q * piece, piece)], o_red.at[0, q], o_red.at[1, q], me.side).start()
        gu_y(1, 3)

        def attend_rows_back(first):
            def one(i, carry):
                toks = pl.ds(pl.multiple_of(first + i * length, length), length)
                tabs = [tab_ref[k] for k in range(3)]
                for j in range(2):
                    q, k, p = probabilities(toks, j)
                    v = heads[toks, (6 + j) * LANES:(7 + j) * LANES]
                    grad = pair(toks, j, mid, 0)
                    d_v = dot_l(low(p), grad)
                    d_p = dot_t(grad, v)
                    d_s = low(p * (d_p - jnp.sum(p * d_p, 1, keepdims=True)))
                    d_q = HD ** (-0.5) * dot32(d_s, k)
                    d_k = HD ** (-0.5) * dot_l(d_s, q)
                    for g in range(2):
                        spot = (2 * j + g) * LANES
                        dgu[0, toks, spot:spot + LANES] = low(turn(d_q[g * length:(g + 1) * length], tabs, -1.0))
                    dgu[0, toks, (4 + j) * LANES:(5 + j) * LANES] = low(turn(d_k, tabs, -1.0))
                    dgu[0, toks, (6 + j) * LANES:(7 + j) * LANES] = low(d_v)
                return carry

            lax.fori_loop(0, rows // length, one, 0)
            toks = pl.ds(pl.multiple_of(first, rows), rows)
            for k in range(2):
                dgu[1, toks, k * heads4:(k + 1) * heads4] = low(
                    dot_t(dgu[0, toks, k * 4 * LANES:(k + 1) * 4 * LANES], sel_ref[...])
                )
            part[toks, :] = low(dot_t(dgu[1, toks, 0:q_cols], qkv_all[...]))

        attend_rows_back((2 * away + 1 - me.c) * rows)
        blocks_start(me, tok(part), got, *h_sems, 0)
        attend_rows_back((2 * away + me.c) * rows)
        blocks_cross(me, tok(part), got, last, *h_sems)
        gu_z(1, 3)
        deal_start(me, finals[1], depth, gu_out.at[1], *gu_deal[1])
        dn_y(0)
        attend_rows_back((2 * home + 1 - me.c) * rows)
        blocks_start(me, tok(part), got, *h_sems, 1)
        attend_rows_back((2 * home + me.c) * rows)
        dn_y(1)
        fetch_n.wait()

        def q_grads(i, carry):
            feats = pl.ds(pl.multiple_of(i * chunk, chunk), chunk)
            qkv_all[feats, :] = low(dot_l(n_buf[:, feats], dgu[1, :, 0:q_cols]))
            return carry

        lax.fori_loop(0, width // chunk, q_grads, 0)
        reduce_start(me, q_slots, q_buf[0], q_sems)
        dn_z(0)
        dn_y(2)

        blocks_finish(me, tok(out_part), got_f, last_f, *f_sems)

        def output(strip):
            got_f[me.s, strip, :] = low(x1[strip, :] + summed(strip, out_part, got_f, last_f))

        strips(rows, output)
        keep_bo = pltpu.make_async_copy(got_f.at[me.s], bo_ref, local.at[1])
        keep_bo.start()
        fetch_x.start()
        dn_z(1)
        dn_z(2)
        dn_y(3)
        reduce_mix(me, q_slots, q_buf[0], q_sems)

        o_sum = lambda q: o_buf[0].at[pl.ds(q * piece, piece)]
        o_left = lambda q: o_buf[1].at[pl.ds(q * piece, piece)]
        o_right = lambda q: o_buf[2].at[pl.ds(q * piece, piece)]

        def o_on(q):
            @pl.when(me.z < me.rank)
            def _():
                push(o_sum(q), o_left(q), o_red.at[4, q], o_red.at[2, q], me.right).start()

            @pl.when(me.z > me.rank)
            def _():
                push(o_sum(q), o_right(q), o_red.at[4, q], o_red.at[3, q], me.left).start()

        from_left = jnp.logical_and(me.has_left, me.z <= me.rank)
        from_right = jnp.logical_and(me.has_right, me.z >= me.rank)
        no_more = jnp.logical_not(jnp.logical_or(from_left, from_right))

        def o_y(q):
            arrived(o_sum(q), o_red.at[1, q], me.side)
            add_into(o_sum(q), bit(me.y, q))

            @pl.when(no_more)
            def _():
                o_on(q)

        def o_z(q):
            @pl.when(from_left)
            def _():
                arrived(o_left(q), o_red.at[2, q], me.left)
                add_into(o_sum(q), o_left(q))

            @pl.when(from_right)
            def _():
                arrived(o_right(q), o_red.at[3, q], me.right)
                add_into(o_sum(q), o_right(q))

            @pl.when(jnp.logical_not(no_more))
            def _():
                o_on(q)

        for q in range(PIECES):
            o_y(q)
        dn_z(3)
        final_dn = dn_buf[0].at[me.z]
        dn_keep, dn_send, dn_recv = dn_deal
        keep_dn = pltpu.make_async_copy(final_dn, dn_out.at[me.s], dn_keep)
        keep_dn.start()
        push(final_dn, dn_out.at[me.s], dn_send, dn_recv, me.across).start()
        o_z(0)
        o_z(1)
        q_y(0)
        o_z(2)
        o_z(3)
        own_half = o_buf[0].at[pl.ds(pl.multiple_of(me.c * head, STRIP), head)]
        other_half = o_buf[0].at[pl.ds(pl.multiple_of((1 - me.c) * head, STRIP), head)]
        o_keep, o_send, o_recv = o_deal
        keep_oo = pltpu.make_async_copy(own_half, out_out, o_keep)

        @pl.when(owner)
        def _():
            keep_oo.start()
            push(other_half, out_out, o_send.at[0], o_recv.at[0], me.core).start()
            push(own_half, out_out, o_send.at[1], o_recv.at[0], me.across).start()
            push(other_half, out_out, o_send.at[2], o_recv.at[0], me.corner).start()

        q_y(1)
        q_z(0)
        q_y(2)

        blocks_finish(me, tok(part), got, last, *h_sems)
        fetch_x.wait()

        def inner(strip):
            got[me.s, strip, :] = low(norm_back(
                last_f[strip, :].astype(F32), summed(strip, part, got, last), dx_all[mine(strip), :].astype(F32)
            ))

        strips(rows, inner)
        keep_gx = pltpu.make_async_copy(got.at[me.s], gx_ref, local.at[2])
        keep_gx.start()
        q_z(1)
        q_z(2)
        q_y(3)
        q_z(3)
        final_q = q_buf[0].at[me.z]
        deal_start(me, final_q, depth, qkv_out, *q_deal)

        for h in range(2):
            reduce_finish(me, own_gu[h], gu_buf[h][0], gu_sems[h])
            deal_finish(me, finals[h], depth, gu_out.at[h], *gu_deal[h])
        reduce_finish(me, dn_slots, dn_buf[0], dn_sems)
        reduce_finish(me, q_slots, q_buf[0], q_sems)
        for q in range(PIECES):
            sum_q = o_sum(q)
            left_over(bit(1 - me.y, q), o_red.at[0, q], me.side)

            @pl.when(me.z < me.rank)
            def _():
                left_over(sum_q, o_red.at[4, q], me.right)

            @pl.when(me.z > me.rank)
            def _():
                left_over(sum_q, o_red.at[4, q], me.left)

        @pl.when(owner)
        def _():
            keep_oo.wait()
            left_over(other_half, o_send.at[0], me.core)
            left_over(own_half, o_send.at[1], me.across)
            left_over(other_half, o_send.at[2], me.corner)

        @pl.when(jnp.logical_not(owner))
        def _():
            arrived(out_out, o_recv.at[0], me.core)

        keep_dn.wait()
        left_over(final_dn, dn_send, me.across)
        arrived(dn_out.at[1 - me.s], dn_recv, me.across)
        keep_bo.wait()
        keep_gx.wait()
        deal_finish(me, final_q, depth, qkv_out, *q_deal)

    sems = lambda *dims: pltpu.SemaphoreType.DMA(dims)
    one, three = pltpu.SemaphoreType.DMA, sems(3)
    vmem = lambda *dims: pltpu.VMEM(dims, BF)
    deal = [one, three, three]
    outs = comm_call(
        kernel, 0,
        [shape((rows, width)), shape((rows, width)), shape((4, depth, q_cols)), shape((head, width)),
         shape((2, 4, depth, cols)), shape((2, block, width)), shape((total, width))],
        [ANY] * 7,
        [(ANY, ref) for ref in (tokens, cot, w_query, w_key, w_value, w_out, w_gate, w_up, w_down)]
        + [(VMEM, gain_attn), (VMEM, gain_mlp), (VMEM, head_tables(length))],
        [vmem(total, width), vmem(total, width), vmem(width, q_cols), vmem(heads4, width), vmem(2, width, cols),
         vmem(units, width), vmem(total, 8 * LANES), vmem(total, heads4)]
        + [vmem(total, width), vmem(total, width), pltpu.VMEM((rows, width), F32), vmem(total, units),
           vmem(2, total, cols), vmem(width, cols), vmem(total, width)]
        + blocks_buffers(rows, width) * 2
        + reduce_buffers(planes, 2 * depth, cols) * 2 + reduce_buffers(planes, block, width)
        + reduce_buffers(planes, 2 * depth, q_cols) + [vmem(2 * head, width)] * 3
        + group_sems() * 4 + blocks_sems() * 4 + [one] * 9
        + line_sems(planes) * 4 + reduce_sems(planes) * 4 + deal * 2 + [one] * 3 + deal * 2
        + [sems(5), sems(2), sems(5, PIECES), sems(5, PIECES), sems(3 + 8 * planes), vmem(heads4, 4 * LANES),
           pltpu.VMEM((2, depth, LANES), F32)],
        "block_step",
    )
    return outs[:6]


def finish(planes, parts, weights, gains):
    block_out, grad_tokens, own_qkv, own_out, own_gu, own_dn = parts
    w_query, w_key, w_value, w_gate, w_up = weights
    rows, width = block_out.shape
    depth, hidden = w_gate.shape
    q_own, k_own = w_query.shape[1] // 4, w_key.shape[1] // 4
    block = own_dn.shape[1]
    steps = 2 * planes
    wide = hidden // steps
    own_dn = own_dn.reshape(2 * block, width)

    def kernel(bo_ref, gx_ref, qkv_ref, out_ref, gate_ref, up_ref, dn_ref, wq_ref, wk_ref, wv_ref, wg_ref, wu_ref,
               ga_ref, gm_ref, bo_out, gx_out, q_out, k_out, v_out, o_out, gate_out, up_out, dn_out, ga_out, gm_out,
               columns, total):
        step = pl.program_id(0)
        same = lax.broadcasted_iota(jnp.int32, (depth, depth), 0) == lax.broadcasted_iota(jnp.int32, (depth, depth), 1)

        def as_row(value):
            return jnp.sum(jnp.where(same, jnp.sum(value, 1, keepdims=True), 0.0), 0, keepdims=True)

        @pl.when(step == 0)
        def _():
            for k, ref in enumerate((ga_ref, gm_ref)):
                column = jnp.sum(jnp.where(same, ref[...].astype(F32), 0.0), 1, keepdims=True)
                columns[k] = jnp.broadcast_to(column, (depth, LANES))
            total[...] = jnp.zeros_like(total)
            o_out[...] = out_ref[...].astype(F32)
            gain = columns[0]
            gathered = jnp.zeros((depth, LANES), F32)

            def put(out, weight, tile, value):
                lanes = slice(tile * LANES, (tile + 1) * LANES)
                out[:, lanes] = value * gain
                return value * weight[:, lanes].astype(F32)

            rolled = lambda value: pltpu.roll(value, LANES // 2, 1)
            in_low = lax.broadcasted_iota(jnp.int32, (depth, LANES), 1) < LANES // 2
            join = lambda first, second: jnp.where(in_low, first, second)
            for rank in range(4):
                for k in range(q_own // LANES):
                    value = qkv_ref[rank, :, k * LANES:(k + 1) * LANES].astype(F32)
                    gathered += put(q_out, wq_ref, rank * q_own // LANES + k, value)
            for seq in range(2):
                (a0, a1, a2), (b0, b1, b2) = [
                    [qkv_ref[2 * seq + core, :, q_own + k * LANES:q_own + (k + 1) * LANES].astype(F32) for k in range(3)]
                    for core in range(2)
                ]
                keys = [a0, join(a1, rolled(b0)), join(rolled(b0), rolled(b1))]
                values = [join(rolled(a1), rolled(a2)), join(rolled(a2), b1), b2]
                for k in range(3):
                    gathered += put(k_out, wk_ref, 3 * seq + k, keys[k])
                    gathered += put(v_out, wv_ref, 3 * seq + k, values[k])
            ga_out[...] = as_row(gathered)

        bo_out[...] = bo_ref[...]
        gx_out[...] = gx_ref[...]
        dn_out[...] = dn_ref[...].astype(F32)
        gain = columns[1]
        gathered = jnp.zeros((depth, LANES), F32)
        for ref, out, weight in ((gate_ref, gate_out, wg_ref), (up_ref, up_out, wu_ref)):
            for core in range(2):
                for seq in range(2):
                    lanes = slice((2 * core + seq) * block, (2 * core + seq + 1) * block)
                    value = ref[0, 2 * seq + core].astype(F32)
                    out[:, lanes] = value * gain
                    gathered += value * weight[:, lanes].astype(F32)
        total[...] += gathered

        @pl.when(step == steps - 1)
        def _():
            gm_out[...] = as_row(total[...])

    whole = lambda ref: pl.BlockSpec(ref.shape, lambda p: (0,) * len(ref.shape))
    strip = lambda ref: pl.BlockSpec((ref.shape[0] // steps, ref.shape[1]), lambda p: (p, 0))
    part = lambda first: pl.BlockSpec((1, 4, depth, block), lambda p: (p // planes, 0, 0, first + p % planes))
    slab = pl.BlockSpec((depth, wide), lambda p: (0, p))
    outs = [shape(block_out.shape), shape(grad_tokens.shape), shape(w_query.shape, F32), shape(w_key.shape, F32),
            shape(w_value.shape, F32), shape(own_out.shape, F32), shape(w_gate.shape, F32), shape(w_up.shape, F32),
            shape(own_dn.shape, F32), shape((1, depth), F32), shape((1, depth), F32)]
    return pl.pallas_call(
        kernel,
        grid=(steps,),
        out_shape=outs,
        in_specs=[strip(block_out), strip(grad_tokens), whole(own_qkv), whole(own_out), part(0), part(planes),
                  strip(own_dn), whole(w_query), whole(w_key), whole(w_value), slab, slab, whole(gains[0]), whole(gains[1])],
        out_specs=[strip(outs[0]), strip(outs[1])] + [whole(o) for o in outs[2:6]]
        + [slab, slab, strip(outs[8]), whole(outs[9]), whole(outs[10])],
        scratch_shapes=[pltpu.VMEM((2, depth, LANES), F32), pltpu.VMEM((depth, LANES), F32)],
        name="finish",
    )(block_out, grad_tokens, own_qkv, own_out, own_gu, own_gu, own_dn, w_query, w_key, w_value, w_gate, w_up, *gains)


def shards_fast(tokens, cotangent, w_query, w_key, w_value, w_out, w_gate, w_up, w_down, gain_attn, gain_mlp):
    seqs, length, width = tokens.shape
    rows = seqs * length
    depth = w_query.shape[0]
    planes = width // depth // 4
    x, cot = tokens.reshape(rows, width), cotangent.reshape(rows, width)
    gains = (gain_attn.reshape(1, depth), gain_mlp.reshape(1, depth))
    parts = block_step(planes, length, x, cot, w_query, w_key, w_value, w_out, w_gate, w_up, w_down, *gains)
    outs = finish(planes, parts, (w_query, w_key, w_value, w_gate, w_up), gains)
    return (
        outs[0].reshape(tokens.shape), outs[1].reshape(tokens.shape), *outs[2:9],
        outs[9].reshape(depth), outs[10].reshape(depth),
    )


def fits(mesh):
    return mesh.shape["seq"] == 2 and mesh.shape["dp"] == 16


def solution(mesh):
    body = shards_fast if fits(mesh) else shards_plain
    return jax.shard_map(body, mesh=mesh, in_specs=IN_SPECS, out_specs=OUT_SPECS, check_vma=False)
```

profile of v0, /device:TPU:0, one launch (start us, length us, event | category | flops | bytes accessed | tf_op | source)
XLA Modules:
  0.0 309.1 jit_solution(3893373897602056195)
XLA Ops:
  0.6 298.7 %block_step.1 = (bf16[256,1536]{1,0:T(8,128)(2,1)}, bf16[256,1536]{1,0:T(8,128)(2,1)}, bf16[4,96,768]{2,1,0:T(8,128)(2,1)}, bf16[96,1536]{1,0:T(8,128)(2,1)}, bf...) custom-call(bf16[256,1536]{1,0:T(8,128)(2,1)} %bitcast.10, ...), custom_call_target="tpu_custom_call" | custom-call | tf_op jit(solution)/shard_map/block_step/pallas_call | solution.py:568
  299.4 9.6 %finish.1 = (bf16[256,1536]{1,0:T(8,128)(2,1)}, bf16[256,1536]{1,0:T(8,128)(2,1)}, f32[96,1536]{1,0:T(8,128)}, f32[96,768]{1,0:T(8,128)}, f32[96,768]{1,0:T(8,12...) custom-call(bf16[256,1536]{1,0:T(8,128)(2,1)} %get-tuple-element.28., ...), custom_call_target="tpu_custom_call" | custom-call | tf_op jit(solution)/shard_map/finish/pallas_call | solution.py:1365
where the time goes:
time: 310 us; the launch traced here: 309 us
  Pallas kernels  308 us (99%)
    pallas_call x1, Pallas kernels, comm_call(): pl.pallas_call(kernel, out_shape=outs, in_specs=[spec for spec, _ in ins]...  299 us
    pallas_call x1, Pallas kernels, finish(): pl.pallas_call(kernel, grid=(steps,), out_shape=outs, in_specs=[strip(blo...  9.57 us

commit v1 on v0

--- a/solution.py
+++ b/solution.py
@@ -1,5 +1,6 @@
 import jax
 import jax.numpy as jnp
+import functools
 import numpy as np
 from jax import lax
 from jax.experimental import pallas as pl
@@ -173,7 +174,7 @@
 F32 = jnp.float32
 STRIP = 16
 PIECES = 4
-VMEM_BYTES = 66_000_000
+VMEM_BYTES = 67_043_328
 
 
 class Place:
@@ -384,12 +385,13 @@
     lax.fori_loop(0, rows // STRIP, body, 0)
 
 
-def reduce_start(me, own, half, sems):
+def reduce_start(me, own, half, sems, which):
     to_side, side, twin = sems[0], sems[1], sems[6]
     orders = far_first(me.planes)
-    away = lower(own(2 * me.twin + 1 - me.y))
-    push(away, lower(half.at[me.z]), twin.at[0], twin.at[1], me.buddy).start()
-    for i in range(me.planes):
+    if 0 in which:
+        away = lower(own(2 * me.twin + 1 - me.y))
+        push(away, lower(half.at[me.z]), twin.at[0], twin.at[1], me.buddy).start()
+    for i in which:
         item = pick([o[i] for o in orders], me.z)
         src, dst = own(2 * item + 1 - me.y), half.at[item]
 
@@ -615,6 +617,19 @@
 def turn(values, tables, sign):
     other = pltpu.roll(values, HD // 2, 1) * tables[1] + pltpu.roll(values, LANES - HD // 2, 1) * tables[2]
     return values * tables[0] + sign * other
+
+
+SCHEDULE = (
+    "De", "Ds", "Q1", "weigh", "Qt", "Q2", "Ae", "D1", "Q3", "rn", "As", "nf", "own", "f0", "f1", "f2", "Qf",
+    "widen", "f3", "A1", "D2", "project", "Be", "oh", "t0", "x0", "Bs", "Dt", "t1", "xc", "D3", "t2", "x1",
+    "A2", "At", "rg", "t3", "xs", "B1", "A3", "Df", "B2", "Bt", "rm", "mf", "Af", "gf", "u0", "B3", "u1",
+    "w0", "ar0", "Bf", "ol", "v0", "v1", "ar1", "b0", "p0", "ay0", "am", "pc", "ay1", "b1", "w1", "br0",
+    "ay2", "az0", "p1", "bs", "br1", "fo", "bm", "by0", "dw", "by1", "rx", "dr0", "az1", "xf", "sp", "fc",
+    "by2", "bz0", "h0", "go", "h1", "dy0", "az2", "oy0", "k0", "dr1", "h2", "kc", "oy1", "bz1", "oy2", "bz2",
+    "h3", "oy3", "qg", "dz0", "ay3", "az3", "by3", "qr0", "dm", "k1", "dy1", "fs", "qr1", "bz3", "be", "oz0",
+    "ae", "qy0", "dy2", "oz1", "oz2", "oz3", "dz1", "oe", "qm", "qy1", "dz2", "qz0", "dy3", "qy2", "dz3",
+    "de", "qy3", "qz1", "qz2", "qz3", "qe", "hs",
+)
 
 
 def block_step(planes, length, tokens, cot, w_query, w_key, w_value, w_out, w_gate, w_up, w_down, gain_attn, gain_mlp):
@@ -754,21 +769,24 @@
         arrived(core_rows(qkv_all)(1 - me.c), q_split[2], me.core)
         line_start(me, q_slots, q_line)
 
-        for copy in units_in:
-            copy.wait()
-
-        def weigh(i, carry):
-            strip = pl.ds(pl.multiple_of(i * STRIP, STRIP), STRIP)
-            gain = gains[1, strip, 0:1]
+        away, home = 1 - me.s, me.s
+
+        def weigh_units():
+            for copy in units_in:
+                copy.wait()
+
+            def weigh(i, carry):
+                strip = pl.ds(pl.multiple_of(i * STRIP, STRIP), STRIP)
+                gain = gains[1, strip, 0:1]
+                for h in range(2):
+                    for ref in (core_rows(gu_all.at[h])(me.c), gu_share[h]):
+                        ref[strip, :] = low(ref[strip, :].astype(F32) * gain)
+                return carry
+
+            lax.fori_loop(0, depth // STRIP, weigh, 0)
             for h in range(2):
-                for ref in (core_rows(gu_all.at[h])(me.c), gu_share[h]):
-                    ref[strip, :] = low(ref[strip, :].astype(F32) * gain)
-            return carry
-
-        lax.fori_loop(0, depth // STRIP, weigh, 0)
-        for h in range(2):
-            push(gu_share[h], core_rows(gu_all.at[h])(me.c), gu_split[h][1], gu_split[h][2], me.core).start()
-        group_start(me, g_loc, tok(g_all), *g_sems)
+                push(gu_share[h], core_rows(gu_all.at[h])(me.c), gu_split[h][1], gu_split[h][2], me.core).start()
+            group_start(me, g_loc, tok(g_all), *g_sems)
 
         fan_in, fan_right, fan_left, fan_side, fan_other = [o_fan.at[k] for k in range(5)]
         bit = lambda y, q: out_all.at[pl.ds(pl.multiple_of(y * 2 * head + q * piece, STRIP), piece)]
@@ -796,66 +814,61 @@
 
             push(mine, mine, fan_side.at[q], fan_other.at[q], me.side).start()
 
-        @pl.when(owner)
-        def _():
-            keep_o.wait()
-            arrived(head_rows(1 - me.c), edge.at[1], me.core)
-
-        @pl.when(lender)
-        def _():
-            left_over(out_loc, edge.at[0], me.core)
-
-        line_hop(me, q_slots, q_line, 1)
-        line_twin(me, q_slots, q_line)
-        fan(0)
-        line_hop(me, q_slots, q_line, 2)
-        group_relay(me, tok(n_buf), *n_sems)
-        fan(1)
-        for hop in range(3, planes):
-            line_hop(me, q_slots, q_line, hop)
-        fan(2)
-        fan(3)
-        arrived(core_rows(gu_all.at[0])(1 - me.c), gu_split[0][2], me.core)
-        line_start(me, gu_slots[0], gu_line[0])
-        keep_d.wait()
-        line_start(me, dn_slots, dn_line)
-        arrived(core_rows(gu_all.at[1])(1 - me.c), gu_split[1][2], me.core)
-        group_finish(me, tok(n_buf).at[me.rank], tok(n_buf), *n_sems)
-        left_over(q_share, q_split[1], me.core)
-        for h in range(2):
-            left_over(gu_share[h], gu_split[h][1], me.core)
+        def own_heads():
+            @pl.when(owner)
+            def _():
+                keep_o.wait()
+                arrived(head_rows(1 - me.c), edge.at[1], me.core)
+
+            @pl.when(lender)
+            def _():
+                left_over(out_loc, edge.at[0], me.core)
+
+        def ends(h):
+            arrived(core_rows(gu_all.at[h])(1 - me.c), gu_split[h][2], me.core)
+            line_ends(me, gu_slots[h], gu_line[h])
+
+        def dn_ends():
+            keep_d.wait()
+            line_ends(me, dn_slots, dn_line)
+
         saved = pltpu.make_async_copy(n_buf, stash, local.at[0])
-        saved.start()
-        line_finish(me, q_slots, q_line)
-
-        def widen(i, carry):
-            feats = pl.ds(pl.multiple_of(i * tile, tile), tile)
-            for k in range(2):
-                g_gu[feats, k * 4 * LANES:(k + 1) * 4 * LANES] = low(
-                    dot32(qkv_all[feats, k * heads4:(k + 1) * heads4], sel_ref[...])
-                )
-            return carry
-
-        lax.fori_loop(0, width // tile, widen, 0)
-
-        def project(i, carry):
-            toks = pl.ds(pl.multiple_of(i * length, length), length)
-            n = n_buf[toks, :]
-            tabs = [tab_ref[k] for k in range(3)]
-            for k in range(8):
-                value = dot32(n, g_gu[:, k * LANES:(k + 1) * LANES])
-                heads[toks, k * LANES:(k + 1) * LANES] = low(turn(value, tabs, 1.0) if k < 6 else value)
-            return carry
-
-        lax.fori_loop(0, total // length, project, 0)
-        line_hop(me, gu_slots[0], gu_line[0], 1)
-        group_relay(me, tok(g_all), *g_sems)
-        line_hop(me, dn_slots, dn_line, 1)
-        line_twin(me, gu_slots[0], gu_line[0])
-        line_twin(me, dn_slots, dn_line)
-        saved.wait()
-        for q in range(PIECES):
-            arrived(bit(1 - me.y, q), fan_other.at[q], me.side)
+        fetch_n = pltpu.make_async_copy(stash, n_buf, local.at[0])
+
+        def normed_here():
+            group_finish(me, tok(n_buf).at[me.rank], tok(n_buf), *n_sems)
+            left_over(q_share, q_split[1], me.core)
+            for h in range(2):
+                left_over(gu_share[h], gu_split[h][1], me.core)
+            saved.start()
+
+        def widen_weights():
+            def widen(i, carry):
+                feats = pl.ds(pl.multiple_of(i * tile, tile), tile)
+                for k in range(2):
+                    g_gu[feats, k * 4 * LANES:(k + 1) * 4 * LANES] = low(
+                        dot32(qkv_all[feats, k * heads4:(k + 1) * heads4], sel_ref[...])
+                    )
+                return carry
+
+            lax.fori_loop(0, width // tile, widen, 0)
+
+        def project_tokens():
+            def project(i, carry):
+                toks = pl.ds(pl.multiple_of(i * length, length), length)
+                n = n_buf[toks, :]
+                tabs = [tab_ref[k] for k in range(3)]
+                for k in range(8):
+                    value = dot32(n, g_gu[:, k * LANES:(k + 1) * LANES])
+                    heads[toks, k * LANES:(k + 1) * LANES] = low(turn(value, tabs, 1.0) if k < 6 else value)
+                return carry
+
+            lax.fori_loop(0, total // length, project, 0)
+
+        def heads_here():
+            saved.wait()
+            for q in range(PIECES):
+                arrived(bit(1 - me.y, q), fan_other.at[q], me.side)
 
         def pair(toks, j, ref, start):
             first = start + 2 * j * LANES
@@ -888,23 +901,6 @@
             toks = pl.ds(pl.multiple_of(first, rows), rows)
             part[toks, :] = low(dot32(mixed[toks, :], out_all[...]))
 
-        away, home = 1 - me.s, me.s
-        attend_rows((2 * away + 1 - me.c) * rows)
-        blocks_start(me, tok(part), got, *x_sems, 0)
-        line_hop(me, gu_slots[0], gu_line[0], 2)
-        line_ends(me, gu_slots[1], gu_line[1])
-        attend_rows((2 * away + me.c) * rows)
-        blocks_cross(me, tok(part), got, last, *x_sems)
-        line_hop(me, dn_slots, dn_line, 2)
-        attend_rows((2 * home + 1 - me.c) * rows)
-        blocks_start(me, tok(part), got, *x_sems, 1)
-        line_side(me, gu_slots[1], gu_line[1])
-        attend_rows((2 * home + me.c) * rows)
-        for hop in range(3, planes):
-            line_hop(me, gu_slots[0], gu_line[0], hop)
-        line_hop(me, gu_slots[1], gu_line[1], 1)
-        blocks_finish(me, tok(part), got, last, *x_sems)
-
         def mine(strip):
             return pl.ds(pl.multiple_of(me.rank * rows + strip.start, STRIP), STRIP)
 
@@ -920,29 +916,26 @@
             x1[strip, :] = value
             n_buf[mine(strip), :] = low(value * inv_rms(value))
 
-        strips(rows, middle)
-        group_start(me, tok(n_buf).at[me.rank], tok(n_buf), *m_sems)
-        for hop in range(3, planes):
-            line_hop(me, dn_slots, dn_line, hop)
-        line_hop(me, gu_slots[1], gu_line[1], 2)
-        line_twin(me, gu_slots[1], gu_line[1])
-        keep_g.wait()
-        group_finish(me, g_loc, tok(g_all), *g_sems)
-        for q in range(PIECES):
-            left_over(bit(me.y, q), fan_side.at[q], me.side)
-
-            @pl.when(go_right)
-            def _():
-                left_over(bit(me.y, q), fan_right.at[q], me.right)
-
-            @pl.when(go_left)
-            def _():
-                left_over(bit(me.y, q), fan_left.at[q], me.left)
-
-        group_relay(me, tok(n_buf), *m_sems)
-        group_finish(me, tok(n_buf).at[me.rank], tok(n_buf), *m_sems)
-        line_finish(me, gu_slots[0], gu_line[0])
-        line_finish(me, dn_slots, dn_line)
+        def first_sum():
+            blocks_finish(me, tok(part), got, last, *x_sems)
+            strips(rows, middle)
+            group_start(me, tok(n_buf).at[me.rank], tok(n_buf), *m_sems)
+
+        def cot_here():
+            keep_g.wait()
+            group_finish(me, g_loc, tok(g_all), *g_sems)
+
+        def heads_left():
+            for q in range(PIECES):
+                left_over(bit(me.y, q), fan_side.at[q], me.side)
+
+                @pl.when(go_right)
+                def _():
+                    left_over(bit(me.y, q), fan_right.at[q], me.right)
+
+                @pl.when(go_left)
+                def _():
+                    left_over(bit(me.y, q), fan_left.at[q], me.left)
 
         def activations(h, j):
             first = h * half_units + j * chunk
@@ -969,26 +962,8 @@
 
             lax.fori_loop(0, width // chunk, step, 0)
 
-        steps = half_units // chunk
-        for j in range(steps):
-            activations(0, j)
-        for hop in range(3, planes):
-            line_hop(me, gu_slots[1], gu_line[1], hop)
-        weight_grads(0, g_gu)
         own_gu = [by_chip(g_gu, 2 * depth), gu_slots[0]]
-        reduce_start(me, own_gu[0], gu_buf[0][0], gu_sems[0])
-        line_finish(me, gu_slots[1], gu_line[1])
-        for j in range(steps):
-            activations(1, j)
         finals = [gu_buf[h][0].at[me.z] for h in range(2)]
-        gu_y = lambda h, i: reduce_y(me, own_gu[h], *gu_buf[h], gu_sems[h], i)
-        gu_z = lambda h, i: reduce_z(me, *gu_buf[h], gu_sems[h], i)
-        gu_mix = lambda h: reduce_mix(me, own_gu[h], gu_buf[h][0], gu_sems[h])
-        dn_y = lambda i: reduce_y(me, dn_slots, *dn_buf, dn_sems, i)
-        dn_z = lambda i: reduce_z(me, *dn_buf, dn_sems, i)
-        q_y = lambda i: reduce_y(me, q_slots, *q_buf, q_sems, i)
-        q_z = lambda i: reduce_z(me, *q_buf, q_sems, i)
-        gu_mix(0)
 
         def back(seq):
             toks = pl.ds(pl.multiple_of(seq * tile, tile), tile)
@@ -1001,73 +976,50 @@
 
             lax.fori_loop(0, width // chunk, step, 0)
 
-        back(away)
-        blocks_start(me, tok(part), got, *b_sems, 0)
-        gu_y(0, 0)
-        back(home)
-        blocks_start(me, tok(part), got, *b_sems, 1)
-        blocks_cross(me, tok(part), got, last, *b_sems)
-
-        weight_grads(1, gu_all.at[0])
-        fetch_n = pltpu.make_async_copy(stash, n_buf, local.at[0])
-        fetch_n.start()
-        reduce_start(me, own_gu[1], gu_buf[1][0], gu_sems[1])
-        gu_y(0, 1)
-        gu_z(0, 0)
-        gu_y(0, 2)
-
-        def forth(i, carry):
-            feats = pl.ds(pl.multiple_of(i * chunk, chunk), chunk)
-            out_part[:, feats] = low(dot32(mid[...], dn_all[:, feats]))
-            return carry
-
-        lax.fori_loop(0, width // chunk, forth, 0)
-        for i in range(2):
-            blocks_start(me, tok(out_part), got_f, *f_sems, i)
-        gu_z(0, 1)
-        gu_z(0, 2)
-        gu_y(0, 3)
-        blocks_finish(me, tok(part), got, last, *b_sems)
+        def second_grads():
+            weight_grads(1, gu_all.at[0])
+            fetch_n.start()
+
+        def outward():
+            def forth(i, carry):
+                feats = pl.ds(pl.multiple_of(i * chunk, chunk), chunk)
+                out_part[:, feats] = low(dot32(mid[...], dn_all[:, feats]))
+                return carry
+
+            lax.fori_loop(0, width // chunk, forth, 0)
+            for i in range(2):
+                blocks_start(me, tok(out_part), got_f, *f_sems, i)
 
         def branch(strip):
             grad = norm_back(x1[strip, :], summed(strip, part, got, last), g_all[mine(strip), :].astype(F32))
             dx_all[mine(strip), :] = low(grad)
 
-        strips(rows, branch)
-        group_start(me, tok(dx_all).at[me.rank], tok(dx_all), *d_sems)
-        gu_mix(1)
-
-        def down(i, carry):
-            these = pl.ds(pl.multiple_of(i * chunk, chunk), chunk)
-            dn_all[these, :] = low(dot_l(mid[:, these], g_all[...]))
-            return carry
-
-        lax.fori_loop(0, units // chunk, down, 0)
-        reduce_start(me, dn_slots, dn_buf[0], dn_sems)
-        gu_z(0, 3)
-        gu_y(1, 0)
-        gu_y(1, 1)
-        gu_z(1, 0)
-        gu_y(1, 2)
-        reduce_mix(me, dn_slots, dn_buf[0], dn_sems)
-        group_relay(me, tok(dx_all), *d_sems)
-        deal_start(me, finals[0], depth, gu_out.at[0], *gu_deal[0])
-        blocks_cross(me, tok(out_part), got_f, last_f, *f_sems)
-        gu_z(1, 1)
-        gu_z(1, 2)
-        group_finish(me, tok(dx_all).at[me.rank], tok(dx_all), *d_sems)
-
-        def spread_out(t, carry):
-            toks = pl.ds(pl.multiple_of(t * rows, rows), rows)
-            grad = low(dot_t(dx_all[toks, :], out_all[...]))
-            mid[toks, 0:4 * LANES] = low(dot32(grad, sel_ref[...]))
-            return carry
-
-        lax.fori_loop(0, 4, spread_out, 0)
-        out_all[...] = low(dot_l(mixed[...], dx_all[...]))
-        for q in range(PIECES):
-            push(bit(1 - me.y, q), o_buf[0].at[pl.ds(q * piece, piece)], o_red.at[0, q], o_red.at[1, q], me.side).start()
-        gu_y(1, 3)
+        def second_sum():
+            blocks_finish(me, tok(part), got, last, *b_sems)
+            strips(rows, branch)
+            group_start(me, tok(dx_all).at[me.rank], tok(dx_all), *d_sems)
+
+        def down_grads():
+            def down(i, carry):
+                these = pl.ds(pl.multiple_of(i * chunk, chunk), chunk)
+                dn_all[these, :] = low(dot_l(mid[:, these], g_all[...]))
+                return carry
+
+            lax.fori_loop(0, units // chunk, down, 0)
+
+        def spread_grads():
+            def spread_out(t, carry):
+                toks = pl.ds(pl.multiple_of(t * rows, rows), rows)
+                grad = low(dot_t(dx_all[toks, :], out_all[...]))
+                mid[toks, 0:4 * LANES] = low(dot32(grad, sel_ref[...]))
+                return carry
+
+            lax.fori_loop(0, 4, spread_out, 0)
+
+        def out_grads():
+            out_all[...] = low(dot_l(mixed[...], dx_all[...]))
+            for q in range(PIECES):
+                push(bit(1 - me.y, q), o_buf[0].at[pl.ds(q * piece, piece)], o_red.at[0, q], o_red.at[1, q], me.side).start()
 
         def attend_rows_back(first):
             def one(i, carry):
@@ -1097,42 +1049,15 @@
                 )
             part[toks, :] = low(dot_t(dgu[1, toks, 0:q_cols], qkv_all[...]))
 
-        attend_rows_back((2 * away + 1 - me.c) * rows)
-        blocks_start(me, tok(part), got, *h_sems, 0)
-        attend_rows_back((2 * away + me.c) * rows)
-        blocks_cross(me, tok(part), got, last, *h_sems)
-        gu_z(1, 3)
-        deal_start(me, finals[1], depth, gu_out.at[1], *gu_deal[1])
-        dn_y(0)
-        attend_rows_back((2 * home + 1 - me.c) * rows)
-        blocks_start(me, tok(part), got, *h_sems, 1)
-        attend_rows_back((2 * home + me.c) * rows)
-        dn_y(1)
-        fetch_n.wait()
-
-        def q_grads(i, carry):
-            feats = pl.ds(pl.multiple_of(i * chunk, chunk), chunk)
-            qkv_all[feats, :] = low(dot_l(n_buf[:, feats], dgu[1, :, 0:q_cols]))
-            return carry
-
-        lax.fori_loop(0, width // chunk, q_grads, 0)
-        reduce_start(me, q_slots, q_buf[0], q_sems)
-        dn_z(0)
-        dn_y(2)
-
-        blocks_finish(me, tok(out_part), got_f, last_f, *f_sems)
-
-        def output(strip):
-            got_f[me.s, strip, :] = low(x1[strip, :] + summed(strip, out_part, got_f, last_f))
-
-        strips(rows, output)
-        keep_bo = pltpu.make_async_copy(got_f.at[me.s], bo_ref, local.at[1])
-        keep_bo.start()
-        fetch_x.start()
-        dn_z(1)
-        dn_z(2)
-        dn_y(3)
-        reduce_mix(me, q_slots, q_buf[0], q_sems)
+        def in_grads():
+            fetch_n.wait()
+
+            def q_grads(i, carry):
+                feats = pl.ds(pl.multiple_of(i * chunk, chunk), chunk)
+                qkv_all[feats, :] = low(dot_l(n_buf[:, feats], dgu[1, :, 0:q_cols]))
+                return carry
+
+            lax.fori_loop(0, width // chunk, q_grads, 0)
 
         o_sum = lambda q: o_buf[0].at[pl.ds(q * piece, piece)]
         o_left = lambda q: o_buf[1].at[pl.ds(q * piece, piece)]
@@ -1174,52 +1099,100 @@
             def _():
                 o_on(q)
 
-        for q in range(PIECES):
-            o_y(q)
-        dn_z(3)
-        final_dn = dn_buf[0].at[me.z]
-        dn_keep, dn_send, dn_recv = dn_deal
-        keep_dn = pltpu.make_async_copy(final_dn, dn_out.at[me.s], dn_keep)
-        keep_dn.start()
-        push(final_dn, dn_out.at[me.s], dn_send, dn_recv, me.across).start()
-        o_z(0)
-        o_z(1)
-        q_y(0)
-        o_z(2)
-        o_z(3)
         own_half = o_buf[0].at[pl.ds(pl.multiple_of(me.c * head, STRIP), head)]
         other_half = o_buf[0].at[pl.ds(pl.multiple_of((1 - me.c) * head, STRIP), head)]
         o_keep, o_send, o_recv = o_deal
         keep_oo = pltpu.make_async_copy(own_half, out_out, o_keep)
 
-        @pl.when(owner)
-        def _():
-            keep_oo.start()
-            push(other_half, out_out, o_send.at[0], o_recv.at[0], me.core).start()
-            push(own_half, out_out, o_send.at[1], o_recv.at[0], me.across).start()
-            push(other_half, out_out, o_send.at[2], o_recv.at[0], me.corner).start()
-
-        q_y(1)
-        q_z(0)
-        q_y(2)
-
-        blocks_finish(me, tok(part), got, last, *h_sems)
-        fetch_x.wait()
+
+        def o_end():
+            @pl.when(owner)
+            def _():
+                keep_oo.start()
+                push(other_half, out_out, o_send.at[0], o_recv.at[0], me.core).start()
+                push(own_half, out_out, o_send.at[1], o_recv.at[0], me.across).start()
+                push(other_half, out_out, o_send.at[2], o_recv.at[0], me.corner).start()
+
+        def output(strip):
+            got_f[me.s, strip, :] = low(x1[strip, :] + summed(strip, out_part, got_f, last_f))
+
+        def third_sum():
+            blocks_finish(me, tok(out_part), got_f, last_f, *f_sems)
+            strips(rows, output)
+            pltpu.make_async_copy(got_f.at[me.s], bo_ref, local.at[1]).start()
+            fetch_x.start()
 
         def inner(strip):
             got[me.s, strip, :] = low(norm_back(
                 last_f[strip, :].astype(F32), summed(strip, part, got, last), dx_all[mine(strip), :].astype(F32)
             ))
 
-        strips(rows, inner)
-        keep_gx = pltpu.make_async_copy(got.at[me.s], gx_ref, local.at[2])
-        keep_gx.start()
-        q_z(1)
-        q_z(2)
-        q_y(3)
-        q_z(3)
-        final_q = q_buf[0].at[me.z]
-        deal_start(me, final_q, depth, qkv_out, *q_deal)
+        def fourth_sum():
+            blocks_finish(me, tok(part), got, last, *h_sems)
+            fetch_x.wait()
+            strips(rows, inner)
+            pltpu.make_async_copy(got.at[me.s], gx_ref, local.at[2]).start()
+
+        final_dn, final_q = dn_buf[0].at[me.z], q_buf[0].at[me.z]
+        dn_keep, dn_send, dn_recv = dn_deal
+
+        def dn_end():
+            pltpu.make_async_copy(final_dn, dn_out.at[me.s], dn_keep).start()
+            push(final_dn, dn_out.at[me.s], dn_send, dn_recv, me.across).start()
+
+        steps = {
+            "weigh": weigh_units, "own": own_heads, "rn": lambda: group_relay(me, tok(n_buf), *n_sems),
+            "Ae": lambda: ends(0), "Be": lambda: ends(1), "De": dn_ends, "nf": normed_here,
+            "widen": widen_weights, "project": project_tokens, "oh": heads_here,
+            "rg": lambda: group_relay(me, tok(g_all), *g_sems), "gf": cot_here, "ol": heads_left,
+            "xs": first_sum, "rm": lambda: group_relay(me, tok(n_buf), *m_sems),
+            "mf": lambda: group_finish(me, tok(n_buf).at[me.rank], tok(n_buf), *m_sems),
+            "w0": lambda: weight_grads(0, g_gu), "w1": second_grads,
+            "b0": lambda: back(away), "b1": lambda: back(home), "fo": outward, "bs": second_sum, "dw": down_grads,
+            "rx": lambda: group_relay(me, tok(dx_all), *d_sems),
+            "xf": lambda: group_finish(me, tok(dx_all).at[me.rank], tok(dx_all), *d_sems),
+            "sp": spread_grads, "go": out_grads, "qg": in_grads, "oe": o_end, "fs": third_sum, "hs": fourth_sum,
+            "fc": lambda: blocks_cross(me, tok(out_part), got_f, last_f, *f_sems),
+            "de": dn_end, "ae": lambda: deal_start(me, finals[0], depth, gu_out.at[0], *gu_deal[0]),
+            "be": lambda: deal_start(me, finals[1], depth, gu_out.at[1], *gu_deal[1]),
+            "qe": lambda: deal_start(me, final_q, depth, qkv_out, *q_deal),
+        }
+        for key, slots, line in (
+            ("Q", q_slots, q_line), ("A", gu_slots[0], gu_line[0]), ("B", gu_slots[1], gu_line[1]), ("D", dn_slots, dn_line)
+        ):
+            steps[key + "s"] = functools.partial(line_side, me, slots, line)
+            steps[key + "t"] = functools.partial(line_twin, me, slots, line)
+            steps[key + "f"] = functools.partial(line_finish, me, slots, line)
+            for hop in range(1, planes):
+                steps[key + str(hop)] = functools.partial(line_hop, me, slots, line, hop)
+        for key, own, buffers, sems in (
+            ("a", own_gu[0], gu_buf[0], gu_sems[0]), ("b", own_gu[1], gu_buf[1], gu_sems[1]),
+            ("d", dn_slots, dn_buf, dn_sems), ("q", q_slots, q_buf, q_sems),
+        ):
+            steps[key + "r0"] = functools.partial(reduce_start, me, own, buffers[0], sems, [0])
+            steps[key + "r1"] = functools.partial(reduce_start, me, own, buffers[0], sems, range(1, planes))
+            steps[key + "m"] = functools.partial(reduce_mix, me, own, buffers[0], sems)
+            for i in range(planes):
+                steps[key + "y" + str(i)] = functools.partial(reduce_y, me, own, *buffers, sems, i)
+                steps[key + "z" + str(i)] = functools.partial(reduce_z, me, *buffers, sems, i)
+        for i in range(PIECES):
+            steps["f" + str(i)] = functools.partial(fan, i)
+            steps["oy" + str(i)] = functools.partial(o_y, i)
+            steps["oz" + str(i)] = functools.partial(o_z, i)
+        for i, (seq, core) in enumerate(((away, 1 - me.c), (away, me.c), (home, 1 - me.c), (home, me.c))):
+            steps["t" + str(i)] = functools.partial(attend_rows, (2 * seq + core) * rows)
+            steps["h" + str(i)] = functools.partial(attend_rows_back, (2 * seq + core) * rows)
+        for key, whole, some, rest, sems in (
+            ("x", part, got, last, x_sems), ("p", part, got, last, b_sems), ("k", part, got, last, h_sems)
+        ):
+            for i in range(2):
+                steps[key + str(i)] = functools.partial(blocks_start, me, tok(whole), some, *sems, i)
+            steps[key + "c"] = functools.partial(blocks_cross, me, tok(whole), some, rest, *sems)
+        for h in range(2):
+            for j in range(half_units // chunk):
+                steps["uv"[h] + str(j)] = functools.partial(activations, h, j)
+        for name in SCHEDULE:
+            steps[name]()
 
         for h in range(2):
             reduce_finish(me, own_gu[h], gu_buf[h][0], gu_sems[h])
@@ -1249,11 +1222,11 @@
         def _():
             arrived(out_out, o_recv.at[0], me.core)
 
-        keep_dn.wait()
+        pltpu.make_async_copy(final_dn, dn_out.at[me.s], dn_keep).wait()
         left_over(final_dn, dn_send, me.across)
         arrived(dn_out.at[1 - me.s], dn_recv, me.across)
-        keep_bo.wait()
-        keep_gx.wait()
+        pltpu.make_async_copy(got_f.at[me.s], bo_ref, local.at[1]).wait()
+        pltpu.make_async_copy(got.at[me.s], gx_ref, local.at[2]).wait()
         deal_finish(me, final_q, depth, qkv_out, *q_deal)
 
     sems = lambda *dims: pltpu.SemaphoreType.DMA(dims)
@@ -1290,7 +1263,8 @@
     depth, hidden = w_gate.shape
     q_own, k_own = w_query.shape[1] // 4, w_key.shape[1] // 4
     block = own_dn.shape[1]
-    steps = 2 * planes
+    per = 4
+    steps = 2 * planes // per
     wide = hidden // steps
     own_dn = own_dn.reshape(2 * block, width)
 
@@ -1343,12 +1317,12 @@
         gain = columns[1]
         gathered = jnp.zeros((depth, LANES), F32)
         for ref, out, weight in ((gate_ref, gate_out, wg_ref), (up_ref, up_out, wu_ref)):
-            for core in range(2):
-                for seq in range(2):
-                    lanes = slice((2 * core + seq) * block, (2 * core + seq + 1) * block)
-                    value = ref[0, 2 * seq + core].astype(F32)
-                    out[:, lanes] = value * gain
-                    gathered += value * weight[:, lanes].astype(F32)
+            for k in range(4 * per):
+                chip, core, seq = k // 4, k // 2 % 2, k % 2
+                lanes = slice(k * block, (k + 1) * block)
+                value = ref[0, 2 * seq + core, :, chip * block:(chip + 1) * block].astype(F32)
+                out[:, lanes] = value * gain
+                gathered += value * weight[:, lanes].astype(F32)
         total[...] += gathered
 
         @pl.when(step == steps - 1)
@@ -1357,7 +1331,8 @@
 
     whole = lambda ref: pl.BlockSpec(ref.shape, lambda p: (0,) * len(ref.shape))
     strip = lambda ref: pl.BlockSpec((ref.shape[0] // steps, ref.shape[1]), lambda p: (p, 0))
-    part = lambda first: pl.BlockSpec((1, 4, depth, block), lambda p: (p // planes, 0, 0, first + p % planes))
+    runs = planes // per
+    part = lambda first: pl.BlockSpec((1, 4, depth, per * block), lambda p: (p // runs, 0, 0, first + p % runs))
     slab = pl.BlockSpec((depth, wide), lambda p: (0, p))
     outs = [shape(block_out.shape), shape(grad_tokens.shape), shape(w_query.shape, F32), shape(w_key.shape, F32),
             shape(w_value.shape, F32), shape(own_out.shape, F32), shape(w_gate.shape, F32), shape(w_up.shape, F32),
@@ -1366,7 +1341,7 @@
         kernel,
         grid=(steps,),
         out_shape=outs,
-        in_specs=[strip(block_out), strip(grad_tokens), whole(own_qkv), whole(own_out), part(0), part(planes),
+        in_specs=[strip(block_out), strip(grad_tokens), whole(own_qkv), whole(own_out), part(0), part(runs),
                   strip(own_dn), whole(w_query), whole(w_key), whole(w_value), slab, slab, whole(gains[0]), whole(gains[1])],
         out_specs=[strip(outs[0]), strip(outs[1])] + [whole(o) for o in outs[2:6]]
         + [slab, slab, strip(outs[8]), whole(outs[9]), whole(outs[10])],

time: 310 us -> 288 us (0.929)
  the two profiles are of different devices: /device:TPU:0 before, /device:TPU:27 now
where the time goes in v1:
time: 288 us; the launch traced here: 287 us
  Pallas kernels  287 us (100%)
    pallas_call x1, Pallas kernels, comm_call(): pl.pallas_call(kernel, out_shape=outs, in_specs=[spec for spec, _ in ins]...  280 us
    pallas_call x1, Pallas kernels, finish(): pl.pallas_call(kernel, grid=(steps,), out_shape=outs, in_specs=[strip(blo...  6.47 us

profile of v1, /device:TPU:27, one launch (start us, length us, event | category | flops | bytes accessed | tf_op | source)
XLA Modules:
  0.0 287.4 jit_solution(13346147261210525485)
XLA Ops:
  0.6 280.1 %block_step.1 = (bf16[256,1536]{1,0:T(8,128)(2,1)}, bf16[256,1536]{1,0:T(8,128)(2,1)}, bf16[4,96,768]{2,1,0:T(8,128)(2,1)}, bf16[96,1536]{1,0:T(8,128)(2,1)}, bf...) custom-call(bf16[256,1536]{1,0:T(8,128)(2,1)} %bitcast.10, ...), custom_call_target="tpu_custom_call" | custom-call | tf_op jit(solution)/shard_map/block_step/pallas_call | solution.py:570
  280.7 6.5 %finish.1 = (bf16[256,1536]{1,0:T(8,128)(2,1)}, bf16[256,1536]{1,0:T(8,128)(2,1)}, f32[96,1536]{1,0:T(8,128)}, f32[96,768]{1,0:T(8,128)}, f32[96,768]{1,0:T(8,12...) custom-call(bf16[256,1536]{1,0:T(8,128)(2,1)} %get-tuple-element.28., ...), custom_call_target="tpu_custom_call" | custom-call | tf_op jit(solution)/shard_map/finish/pallas_call | solution.py:1340

commit v2 on v1

--- a/solution.py
+++ b/solution.py
@@ -201,7 +201,10 @@
     barrier = pltpu.get_barrier_semaphore()
     for peer in (me.core, me.across, me.corner, me.side, me.right, me.left):
         pl.semaphore_signal(barrier, inc=1, device_id=peer, device_id_type=MESH)
-    pl.semaphore_wait(barrier, 6)
+
+
+def met():
+    pl.semaphore_wait(pltpu.get_barrier_semaphore(), 6)
 
 
 def push(src, dst, send, recv, peer):
@@ -620,15 +623,16 @@
 
 
 SCHEDULE = (
-    "De", "Ds", "Q1", "weigh", "Qt", "Q2", "Ae", "D1", "Q3", "rn", "As", "nf", "own", "f0", "f1", "f2", "Qf",
-    "widen", "f3", "A1", "D2", "project", "Be", "oh", "t0", "x0", "Bs", "Dt", "t1", "xc", "D3", "t2", "x1",
-    "A2", "At", "rg", "t3", "xs", "B1", "A3", "Df", "B2", "Bt", "rm", "mf", "Af", "gf", "u0", "B3", "u1",
-    "w0", "ar0", "Bf", "ol", "v0", "v1", "ar1", "b0", "p0", "ay0", "am", "pc", "ay1", "b1", "w1", "br0",
-    "ay2", "az0", "p1", "bs", "br1", "fo", "bm", "by0", "dw", "by1", "rx", "dr0", "az1", "xf", "sp", "fc",
-    "by2", "bz0", "h0", "go", "h1", "dy0", "az2", "oy0", "k0", "dr1", "h2", "kc", "oy1", "bz1", "oy2", "bz2",
-    "h3", "oy3", "qg", "dz0", "ay3", "az3", "by3", "qr0", "dm", "k1", "dy1", "fs", "qr1", "bz3", "be", "oz0",
-    "ae", "qy0", "dy2", "oz1", "oz2", "oz3", "dz1", "oe", "qm", "qy1", "dz2", "qz0", "dy3", "qy2", "dz3",
-    "de", "qy3", "qz1", "qz2", "qz3", "qe", "hs",
+    "weigh", "Q1", "De", "Q2", "Ae", "Qt", "As", "Q3", "own", "Ds", "f0", "f1", "f2", "f3", "D1", "Qf", "Be",
+    "rn", "Bs", "widen", "nf", "project", "oh", "D2", "A1", "t0", "x0", "t1", "xc", "rg", "t2", "x1", "ol",
+    "t3", "gf", "At", "D3", "A2", "xs", "A3", "B1", "Dt", "B2", "rm", "Af", "mf", "Bt", "Df", "u0", "B3",
+    "u1", "w0", "ar0", "ar1", "Bf", "v0", "v1", "b0", "p0", "ay0", "am", "pc", "b1", "ay1", "p1", "w1", "ay2",
+    "br0", "fo", "br1", "az0", "bs", "dw", "by0", "az1", "az2", "bm", "ay3", "by1", "by2", "rx", "az3", "xf",
+    "fc", "dr0", "ae", "sp", "go", "bz0", "h0", "h1", "dr1", "k0", "dy0", "bz1", "h2", "oy0", "k1", "oy1",
+    "bz2", "kc", "by3", "oy2", "h3", "oy3", "qg", "qr0", "qr1", "jr0", "oz0", "dm", "dy1", "oz1", "bz3", "be",
+    "jr1", "oz2", "qy0", "oz3", "oe", "dz0", "qm", "dy2", "dy3", "dz1", "dz2", "jy0", "jm", "qy1", "qz0",
+    "fs", "jy1", "qy2", "dz3", "jz0", "de", "jy2", "qz1", "qz2", "qy3", "jz1", "jz2", "qz3", "qe", "jy3",
+    "jz3", "je", "hs",
 )
 
 
@@ -654,12 +658,12 @@
         n_buf, g_all, qkv_all, out_all, gu_all, dn_all, heads, mixed = take(8)
         part, out_part, x1, mid, dgu, g_gu, dx_all = take(7)
         (got, last), (got_f, last_f) = take(2), take(2)
-        gu_buf, dn_buf, q_buf, o_buf = [take(2), take(2)], take(2), take(2), take(3)
+        gu_buf, dn_buf, q_buf, o_buf = [take(2), take(2)], take(2), [take(2), take(2)], take(3)
         n_sems, g_sems, m_sems, d_sems = take(2), take(2), take(2), take(2)
         x_sems, b_sems, f_sems, h_sems = take(2), take(2), take(2), take(2)
         q_split, gu_split = take(3), [take(3), take(3)]
         q_line, gu_line, dn_line = take(6), [take(6), take(6)], take(6)
-        gu_sems, dn_sems, q_sems = [take(7), take(7)], take(7), take(7)
+        gu_sems, dn_sems, q_sems = [take(7), take(7)], take(7), [take(7), take(7)]
         gu_deal, dn_deal, q_deal, o_deal = [take(3), take(3)], take(3), take(3), take(3)
         local, edge, o_fan, o_red, fetch, sel_ref, gains = take(7)
         me = Place(planes)
@@ -682,7 +686,7 @@
             heads_in.append(pltpu.make_async_copy(src, stage.at[:, pl.ds(spot, size)], fetch.at[i]))
             heads_in[-1].start()
 
-        q_share = q_buf[0].at[0, pl.ds(0, depth)]
+        q_share = q_buf[0][0].at[0]
         gu_share = [mid.at[pl.ds(h * depth, depth)] for h in range(2)]
         units_in = []
         for other in range(2):
@@ -742,6 +746,7 @@
             def _():
                 q_share[...] = value
 
+        met()
         push(q_share, core_rows(qkv_all)(me.c), q_split[1], q_split[2], me.core).start()
         here = me.s == me.z // 2
         owner = me.z == me.rank
@@ -1133,7 +1138,24 @@
             strips(rows, inner)
             pltpu.make_async_copy(got.at[me.s], gx_ref, local.at[2]).start()
 
-        final_dn, final_q = dn_buf[0].at[me.z], q_buf[0].at[me.z]
+        final_dn = dn_buf[0].at[me.z]
+        final_q = [q_buf[k][0].at[me.z] for k in range(2)]
+        own_q = [functools.partial(lambda k, chip: core_rows_of(chip, k), k) for k in range(2)]
+        q_keep, q_send, q_recv = q_deal
+
+        def core_rows_of(chip, core):
+            return qkv_all.at[pl.ds(pl.multiple_of((2 * chip + core) * depth, STRIP), depth)]
+
+        def q_end(core):
+            @pl.when(me.c == core)
+            def _():
+                pltpu.make_async_copy(final_q[core], qkv_out.at[me.rank], q_keep).start()
+                push(final_q[core], qkv_out.at[me.rank], q_send.at[0], q_recv.at[0], me.across).start()
+
+            @pl.when(me.c != core)
+            def _():
+                push(final_q[core], qkv_out.at[me.rank], q_send.at[1], q_recv.at[1], me.core).start()
+                push(final_q[core], qkv_out.at[me.rank], q_send.at[2], q_recv.at[2], me.corner).start()
         dn_keep, dn_send, dn_recv = dn_deal
 
         def dn_end():
@@ -1155,7 +1177,7 @@
             "fc": lambda: blocks_cross(me, tok(out_part), got_f, last_f, *f_sems),
             "de": dn_end, "ae": lambda: deal_start(me, finals[0], depth, gu_out.at[0], *gu_deal[0]),
             "be": lambda: deal_start(me, finals[1], depth, gu_out.at[1], *gu_deal[1]),
-            "qe": lambda: deal_start(me, final_q, depth, qkv_out, *q_deal),
+            "qe": lambda: q_end(0), "je": lambda: q_end(1),
         }
         for key, slots, line in (
             ("Q", q_slots, q_line), ("A", gu_slots[0], gu_line[0]), ("B", gu_slots[1], gu_line[1]), ("D", dn_slots, dn_line)
@@ -1167,7 +1189,7 @@
                 steps[key + str(hop)] = functools.partial(line_hop, me, slots, line, hop)
         for key, own, buffers, sems in (
             ("a", own_gu[0], gu_buf[0], gu_sems[0]), ("b", own_gu[1], gu_buf[1], gu_sems[1]),
-            ("d", dn_slots, dn_buf, dn_sems), ("q", q_slots, q_buf, q_sems),
+            ("d", dn_slots, dn_buf, dn_sems), ("q", own_q[0], q_buf[0], q_sems[0]), ("j", own_q[1], q_buf[1], q_sems[1]),
         ):
             steps[key + "r0"] = functools.partial(reduce_start, me, own, buffers[0], sems, [0])
             steps[key + "r1"] = functools.partial(reduce_start, me, own, buffers[0], sems, range(1, planes))
@@ -1198,7 +1220,8 @@
             reduce_finish(me, own_gu[h], gu_buf[h][0], gu_sems[h])
             deal_finish(me, finals[h], depth, gu_out.at[h], *gu_deal[h])
         reduce_finish(me, dn_slots, dn_buf[0], dn_sems)
-        reduce_finish(me, q_slots, q_buf[0], q_sems)
+        for k in range(2):
+            reduce_finish(me, own_q[k], q_buf[k][0], q_sems[k])
         for q in range(PIECES):
             sum_q = o_sum(q)
             left_over(bit(1 - me.y, q), o_red.at[0, q], me.side)
@@ -1227,7 +1250,22 @@
         arrived(dn_out.at[1 - me.s], dn_recv, me.across)
         pltpu.make_async_copy(got_f.at[me.s], bo_ref, local.at[1]).wait()
         pltpu.make_async_copy(got.at[me.s], gx_ref, local.at[2]).wait()
-        deal_finish(me, final_q, depth, qkv_out, *q_deal)
+
+        for core in range(2):
+
+            @pl.when(me.c == core)
+            def _():
+                pltpu.make_async_copy(final_q[core], qkv_out.at[me.rank], q_keep).wait()
+                left_over(final_q[core], q_send.at[0], me.across)
+
+            @pl.when(me.c != core)
+            def _():
+                left_over(final_q[core], q_send.at[1], me.core)
+                left_over(final_q[core], q_send.at[2], me.corner)
+
+        arrived(qkv_out.at[2 * (1 - me.s) + me.c], q_recv.at[0], me.across)
+        arrived(qkv_out.at[2 * me.s + 1 - me.c], q_recv.at[1], me.core)
+        arrived(qkv_out.at[2 * (1 - me.s) + 1 - me.c], q_recv.at[2], me.corner)
 
     sems = lambda *dims: pltpu.SemaphoreType.DMA(dims)
     one, three = pltpu.SemaphoreType.DMA, sems(3)
@@ -1246,9 +1284,9 @@
            vmem(2, total, cols), vmem(width, cols), vmem(total, width)]
         + blocks_buffers(rows, width) * 2
         + reduce_buffers(planes, 2 * depth, cols) * 2 + reduce_buffers(planes, block, width)
-        + reduce_buffers(planes, 2 * depth, q_cols) + [vmem(2 * head, width)] * 3
+        + reduce_buffers(planes, depth, q_cols) * 2 + [vmem(2 * head, width)] * 3
         + group_sems() * 4 + blocks_sems() * 4 + [one] * 9
-        + line_sems(planes) * 4 + reduce_sems(planes) * 4 + deal * 2 + [one] * 3 + deal * 2
+        + line_sems(planes) * 4 + reduce_sems(planes) * 5 + deal * 2 + [one] * 3 + deal * 2
         + [sems(5), sems(2), sems(5, PIECES), sems(5, PIECES), sems(3 + 8 * planes), vmem(heads4, 4 * LANES),
            pltpu.VMEM((2, depth, LANES), F32)],
         "block_step",

time: 288 us -> 286 us (level)
  Pallas kernels: 287 us -> 282 us
    pallas_call x1, Pallas kernels: 280 us -> 276 us  [comm_call(): pl.pallas_call(kernel, out_shape=outs, in_specs=[spec for spec, _ in ins]...]
where the time goes in v2:
time: 286 us; the launch traced here: 283 us
  Pallas kernels  282 us (99%)
    pallas_call x1, Pallas kernels, comm_call(): pl.pallas_call(kernel, out_shape=outs, in_specs=[spec for spec, _ in ins]...  276 us
    pallas_call x1, Pallas kernels, finish(): pl.pallas_call(kernel, grid=(steps,), out_shape=outs, in_specs=[strip(blo...  6.47 us

profile of v2, /device:TPU:27, one launch (start us, length us, event | category | flops | bytes accessed | tf_op | source)
XLA Modules:
  0.0 283.0 jit_solution(2701706035964888403)
XLA Ops:
  0.6 275.7 %block_step.1 = (bf16[256,1536]{1,0:T(8,128)(2,1)}, bf16[256,1536]{1,0:T(8,128)(2,1)}, bf16[4,96,768]{2,1,0:T(8,128)(2,1)}, bf16[96,1536]{1,0:T(8,128)(2,1)}, bf...) custom-call(bf16[256,1536]{1,0:T(8,128)(2,1)} %bitcast.10, ...), custom_call_target="tpu_custom_call" | custom-call | tf_op jit(solution)/shard_map/block_step/pallas_call | solution.py:573
  276.3 6.5 %finish.1 = (bf16[256,1536]{1,0:T(8,128)(2,1)}, bf16[256,1536]{1,0:T(8,128)(2,1)}, f32[96,1536]{1,0:T(8,128)}, f32[96,768]{1,0:T(8,128)}, f32[96,768]{1,0:T(8,12...) custom-call(bf16[256,1536]{1,0:T(8,128)(2,1)} %get-tuple-element.28., ...), custom_call_target="tpu_custom_call" | custom-call | tf_op jit(solution)/shard_map/finish/pallas_call | solution.py:1378

commit v3 on v2

--- a/solution.py
+++ b/solution.py
@@ -623,16 +623,16 @@
 
 
 SCHEDULE = (
-    "weigh", "Q1", "De", "Q2", "Ae", "Qt", "As", "Q3", "own", "Ds", "f0", "f1", "f2", "f3", "D1", "Qf", "Be",
-    "rn", "Bs", "widen", "nf", "project", "oh", "D2", "A1", "t0", "x0", "t1", "xc", "rg", "t2", "x1", "ol",
-    "t3", "gf", "At", "D3", "A2", "xs", "A3", "B1", "Dt", "B2", "rm", "Af", "mf", "Bt", "Df", "u0", "B3",
-    "u1", "w0", "ar0", "ar1", "Bf", "v0", "v1", "b0", "p0", "ay0", "am", "pc", "b1", "ay1", "p1", "w1", "ay2",
-    "br0", "fo", "br1", "az0", "bs", "dw", "by0", "az1", "az2", "bm", "ay3", "by1", "by2", "rx", "az3", "xf",
-    "fc", "dr0", "ae", "sp", "go", "bz0", "h0", "h1", "dr1", "k0", "dy0", "bz1", "h2", "oy0", "k1", "oy1",
-    "bz2", "kc", "by3", "oy2", "h3", "oy3", "qg", "qr0", "qr1", "jr0", "oz0", "dm", "dy1", "oz1", "bz3", "be",
-    "jr1", "oz2", "qy0", "oz3", "oe", "dz0", "qm", "dy2", "dy3", "dz1", "dz2", "jy0", "jm", "qy1", "qz0",
-    "fs", "jy1", "qy2", "dz3", "jz0", "de", "jy2", "qz1", "qz2", "qy3", "jz1", "jz2", "qz3", "qe", "jy3",
-    "jz3", "je", "hs",
+    "weigh", "Q1", "Ae", "Q2", "As", "rn", "own", "f0", "f1", "f2", "Qt", "Q3", "f3", "A1", "De", "Be", "Qf",
+    "Bs", "Ds", "widen", "nf", "project", "D1", "oh", "t0", "x0", "t1", "xc", "A2", "t2", "D2", "rg", "x1",
+    "t3", "Dt", "A3", "At", "xs", "gf", "ol", "B1", "D3", "B2", "rm", "Af", "Df", "Bt", "mf", "u0", "B3",
+    "u1", "w0", "ar0", "ar1", "Bf", "v0", "v1", "b0", "p0", "ay0", "am", "pc", "ay1", "b1", "p1", "w1", "br0",
+    "az0", "ay2", "bs", "br1", "fo", "by0", "dw", "dr0", "az1", "ay3", "bm", "by1", "az2", "rx", "by2", "xf",
+    "fc", "sp", "go", "bz0", "h0", "k0", "dy0", "az3", "h1", "dr1", "oy0", "kc", "bz1", "oy1", "bz2", "h2",
+    "by3", "k1", "oy2", "ae", "oy3", "dm", "h3", "dz0", "dy1", "qg", "qr0", "jr0", "dy2", "oz0", "bz3", "be",
+    "qr1", "oz1", "oz2", "jr1", "qy0", "oz3", "oe", "dz1", "jy0", "jm", "dy3", "dz2", "qm", "fs", "jy1",
+    "qz0", "qy1", "jz0", "dz3", "jy2", "de", "qy2", "jy3", "jz1", "jz2", "qz1", "qy3", "hs", "qz2", "jz3",
+    "je", "qz3", "qe",
 )
 
 

time: 286 us -> 287 us (level)
  no operation moved by 1% of the time
where the time goes in v3:
time: 287 us; the launch traced here: 282 us
  Pallas kernels  281 us (98%)
    pallas_call x1, Pallas kernels, comm_call(): pl.pallas_call(kernel, out_shape=outs, in_specs=[spec for spec, _ in ins]...  275 us
    pallas_call x1, Pallas kernels, finish(): pl.pallas_call(kernel, grid=(steps,), out_shape=outs, in_specs=[strip(blo...  6.47 us

profile of v3, /device:TPU:27, one launch (start us, length us, event | category | flops | bytes accessed | tf_op | source)
XLA Modules:
  0.0 282.2 jit_solution(5634691199717848546)
XLA Ops:
  0.6 274.9 %block_step.1 = (bf16[256,1536]{1,0:T(8,128)(2,1)}, bf16[256,1536]{1,0:T(8,128)(2,1)}, bf16[4,96,768]{2,1,0:T(8,128)(2,1)}, bf16[96,1536]{1,0:T(8,128)(2,1)}, bf...) custom-call(bf16[256,1536]{1,0:T(8,128)(2,1)} %bitcast.10, ...), custom_call_target="tpu_custom_call" | custom-call | tf_op jit(solution)/shard_map/block_step/pallas_call | solution.py:573
  275.6 6.5 %finish.1 = (bf16[256,1536]{1,0:T(8,128)(2,1)}, bf16[256,1536]{1,0:T(8,128)(2,1)}, f32[96,1536]{1,0:T(8,128)}, f32[96,768]{1,0:T(8,128)}, f32[96,768]{1,0:T(8,12...) custom-call(bf16[256,1536]{1,0:T(8,128)(2,1)} %get-tuple-element.28., ...), custom_call_target="tpu_custom_call" | custom-call | tf_op jit(solution)/shard_map/finish/pallas_call | solution.py:1378
